TPU v7x, 32 devices: a whole 2x2x4 slice. The times are simulated.
32 devices in a mesh: dp: 4 (over z), tensor: 8 (over y, x, core).
Axes of the slice: x: 2, y: 2, z: 4, core: 2. Of those that a mesh axis runs over, the one named last changes fastest.
Arguments:
- activations: bfloat16 [16384, 4096], P(('dp', 'tensor')), may hold values from -6 to 6
- cotangent: bfloat16 [16384, 11008], P('dp', 'tensor'), may hold values from -0.016357422 to 0.016357422
- projection: bfloat16 [4096, 512], replicated, may hold values from -0.25 to 0.25
- first_moment: float32 [512, 11008], P('dp', 'tensor'), may hold values from -0.6 to 0.6
- second_moment: float32 [512, 11008], P('dp', 'tensor'), may hold values from 0.01 to 1
- step_count: int32 [1], replicated, may hold values from 1 to 39
Outputs:
- update: bfloat16 [4096, 11008], P('dp', 'tensor')
- new_first: float32 [512, 11008], P('dp', 'tensor')
- new_second: float32 [512, 11008], P('dp', 'tensor')
All inputs are finite; a program needn't handle non-finite values.
Results may differ from a plain program's by a relative error of at most 0.0055.
Values may be sent and summed in bfloat16 or wider, within the bound.
No kernel may reach another device: no remote copies, remote signals or barrier semaphores. Data moves between devices by JAX's collectives and lax.ppermute only.
A program may use at most 128 MiB of HBM per device.

v0:
```python
import jax
import jax.numpy as jnp
from jax import lax
from jax.sharding import PartitionSpec as P


def per_device(activations, cotangent, projection, first_moment, second_moment, step_count):
    projected = jnp.dot(activations, projection, preferred_element_type=jnp.float32).astype(
        jnp.bfloat16
    )
    width = projection.shape[0]
    replica = lax.axis_index("dp")
    partial_grad = lax.dot_general(
        lax.all_gather(projected, "tensor", axis=0, tiled=True),
        cotangent,
        (((0,), (0,)), ((), ())),
        preferred_element_type=jnp.float32,
    )
    grad = lax.psum_scatter(partial_grad, "dp", scatter_dimension=0, tiled=True)
    t_value = step_count[0].astype(jnp.float32)
    new_first = 0.9 * first_moment + 0.1 * grad
    new_second = 0.999 * second_moment + 0.001 * grad * grad
    first_hat = new_first / (1.0 - jnp.power(jnp.float32(0.9), t_value))
    second_hat = new_second / (1.0 - jnp.power(jnp.float32(0.999), t_value))
    normalized = (first_hat / (jnp.sqrt(second_hat) + 1e-08)).astype(jnp.bfloat16)
    whole_steps = lax.all_gather(normalized, "dp", axis=0, tiled=True)
    out_rows = width // lax.axis_size("dp")
    local_projection = lax.dynamic_slice_in_dim(projection, replica * out_rows, out_rows, 0)
    update = jnp.dot(local_projection, whole_steps, preferred_element_type=jnp.float32).astype(
        jnp.bfloat16
    )
    return (update, new_first, new_second)


def solution(mesh):
    in_specs = (
        P(("dp", "tensor"), None),
        P("dp", "tensor"),
        P(),
        P("dp", "tensor"),
        P("dp", "tensor"),
        P(),
    )
    out_specs = (P("dp", "tensor"), P("dp", "tensor"), P("dp", "tensor"))
    return jax.shard_map(
        per_device, mesh=mesh, in_specs=in_specs, out_specs=out_specs, check_vma=False
    )
```

profile of v0, /device:TPU:0, one launch (start us, length us, event | category | flops | bytes accessed | tf_op | source)
XLA Modules:
  0.0 168.8 jit_solution(3553119309900874069)
XLA Ops:
  7.2 0.0 all-gather.3.cloned.1.call-start
  7.2 6.6 %convolution_convert_fusion.1 = bf16[512,512]{1,0:T(8,128)(2,1)} fusion(bf16[512,4096]{1,0:T(8,128)(2,1)} %param.6, bf16[4096,512]{1,0:T(8,128)(2,1)} %param.8), kind=kOutput, calls=%fused_computation.1 | convolution fusion | flops 2147745792 | bytes 8912896 | tf_op jit(solution)/shard_map/dot_general | solution.py:8
  13.8 0.0 all-gather.3.cloned.1.call-update
  13.8 0.0 copy-start
  13.8 0.0 copy-start.1
  13.9 0.0 reduce-scatter.2.cloned.1.call-start
  13.9 39.4 %all-gather.3.cloned.1.call-done = bf16[4096,512]{1,0:T(8,128)(2,1)} async-done(((bf16[512,512]{1,0:T(8,128)(2,1)}), bf16[4096,512]{1,0:T(8,128)(2,1)}) %all-gather.3.cloned.1.call-update) | async-done | bytes 4194320 | tf_op jit(solution)/shard_map/all_gather | solution.py:14
  53.3 11.1 %fusion.4 = f32[512,1376]{0,1:T(8,128)} fusion(bf16[4096,1376]{0,1:T(8,128)(2,1)} %param.7, bf16[4096,512]{1,0:T(8,128)(2,1)} %all-gather.3.cloned.1.call-done), kind=kOutput, calls=%fused_computation.8 | convolution fusion | flops 5771362304 | bytes 18284544 | tf_op jit(solution)/shard_map/dot_general | solution.py:13
  64.4 0.0 reduce-scatter.2.cloned.1.call-update
  64.4 0.0 all-gather.5.cloned.1.call-start
  65.2 54.7 %reduce-scatter.2.cloned.1.call-done = f32[128,1376]{0,1:T(8,128)} async-done(((f32[512,1376]{0,1:T(8,128)}), f32[128,1376]{0,1:T(8,128)}) %reduce-scatter.2.cloned.1.call-update) | async-done | bytes 704528 | tf_op jit(solution)/shard_map/reduce_scatter | solution.py:19
  119.9 0.0 copy-done
  119.9 0.0 copy-done.1
  119.9 2.5 %divide_convert_fusion = (bf16[128,1376]{0,1:T(8,128)(2,1)}, f32[128,1376]{0,1:T(8,128)}, f32[128,1376]{0,1:T(8,128)}) fusion(f32[]{:T(128)} %bitcast.1, f32[]{:T(128)} %bitcast, f32[128,1376]{0,1:T(8,128)} %reduce-scatter.2.cloned.1.call-done, f32[128,1376]{0,1:T(8,128)S(1)} %copy-done, f32[128,1376]{0,1:T(8,128)S(1)} %copy-done.1), kind=kLoop, calls=%fused_computation.5 | loop fusion | flops 2113536 | bytes 3874824 | tf_op jit(solution)/shard_map/convert_element_type | solution.py:25
  122.4 0.0 all-gather.5.cloned.1.call-update
  122.4 34.9 %all-gather.5.cloned.1.call-done = bf16[512,1376]{0,1:T(8,128)(2,1)} async-done(((bf16[128,1376]{0,1:T(8,128)(2,1)}), bf16[512,1376]{0,1:T(8,128)(2,1)}) %all-gather.5.cloned.1.call-update) | async-done | bytes 1409040 | tf_op jit(solution)/shard_map/all_gather | solution.py:26
  157.4 4.9 %convolution_convert_fusion = bf16[1024,1376]{0,1:T(8,128)(2,1)} fusion(bf16[512,1376]{0,1:T(8,128)(2,1)} %all-gather.5.cloned.1.call-done, bf16[4096,512]{1,0:T(8,128)(2,1)} %param.8, s32[]{:T(128)S(6)} %select_n.3), kind=kOutput, calls=%fused_computation | convolution fusion | flops 1444249600 | bytes 5275652 | tf_op jit(solution)/shard_map/dot_general | solution.py:29
Async XLA Ops:
  7.2 46.1 %all-gather.3.cloned.1.call-start = ((), (), s32[]{:S(2)}) async-start(), calls=%async_computation.1 | async-start | bytes 4718592 | tf_op jit(solution)/shard_map/all_gather | solution.py:14
  13.8 106.0 %copy-start = (f32[128,1376]{0,1:T(8,128)S(1)}, f32[128,1376]{0,1:T(8,128)}, u32[]{:S(2)}) copy-start(f32[128,1376]{0,1:T(8,128)} %param.10) | copy-start | bytes 2113540
  13.8 106.0 %copy-start.1 = (f32[128,1376]{0,1:T(8,128)S(1)}, f32[128,1376]{0,1:T(8,128)}, u32[]{:S(2)}) copy-start(f32[128,1376]{0,1:T(8,128)} %param.9) | copy-start | bytes 2113540
  13.9 106.0 %reduce-scatter.2.cloned.1.call-start = ((), (), s32[]{:S(2)}) async-start(), calls=%async_computation.2 | async-start | bytes 3522560 | tf_op jit(solution)/shard_map/reduce_scatter | solution.py:19
  64.4 93.0 %all-gather.5.cloned.1.call-start = ((), (), s32[]{:S(2)}) async-start(), calls=%async_computation.3 | async-start | bytes 1761280 | tf_op jit(solution)/shard_map/all_gather | solution.py:26
Sparse Core Ops, SparseCore 0:
  13.9 39.2 all-gather.2
  64.5 55.2 reduce-scatter.1
  122.5 34.7 all-gather.4
where the time goes:
time: 169 us
  waiting for transfers between devices  129 us (76%)
  matrix products  22.6 us (13%)
  between operations  14.5 us (9%)
  other arithmetic  2.55 us (2%)
    reduce_scatter x1, waiting for transfers between devices, per_device(): grad = lax.psum_scatter(partial_grad, 'dp', scatter_dimension=0, tiled=True)  54.7 us
    all_gather x1, waiting for transfers between devices, per_device(): lax.all_gather(projected, 'tensor', axis=0, tiled=True)  39.4 us
    all_gather x1, waiting for transfers between devices, per_device(): whole_steps = lax.all_gather(normalized, 'dp', axis=0, tiled=True)  34.9 us
    dot_general x1, matrix products, per_device(): lax.dot_general(lax.all_gather(projected, 'tensor', axis=0, tiled=True),...  11.1 us
    dot_general x1, matrix products, per_device(): jnp.dot(activations, projection, preferred_element_type=jnp.float32)  6.59 us
    dot_general x1, matrix products, per_device(): jnp.dot(local_projection, whole_steps, preferred_element_type=jnp.float32)  4.89 us
  transfers between devices with their start and end apart: 3, of which 3 were waited for; matrix products, arithmetic and copies ran while one was open for 0% of the time, Pallas kernels for 0%

commit v1 on v0

v1 whole, which is shorter than its diff:
```python
import jax
import jax.numpy as jnp
import numpy as np
from jax import lax
from jax.experimental import pallas as pl
from jax.experimental.pallas import tpu as pltpu
from jax.sharding import PartitionSpec as P


F32 = jnp.float32
BF16 = jnp.bfloat16
PROJECT_VMEM = 51 << 20
TOKEN_VMEM = 16 << 20
APPLY_VMEM = 12 << 20
SMALL_VMEM = 4 << 20
LOAD_VMEM = 47 << 20
TOKEN_TILE = 344
LANES = 128


def adam(grad, first_moment, second_moment, step_count):
    t_value = step_count[0].astype(F32)
    new_first = 0.9 * first_moment + 0.1 * grad
    new_second = 0.999 * second_moment + 0.001 * grad * grad
    first_hat = new_first / (1.0 - jnp.power(F32(0.9), t_value))
    second_hat = new_second / (1.0 - jnp.power(F32(0.999), t_value))
    normalized = (first_hat / (jnp.sqrt(second_hat) + 1e-08)).astype(BF16)
    return new_first, new_second, normalized


def plain(activations, cotangent, projection, first_moment, second_moment, step_count):
    projected = jnp.dot(activations, projection, preferred_element_type=F32).astype(BF16)
    partial_grad = lax.dot_general(
        lax.all_gather(projected, "tensor", axis=0, tiled=True),
        cotangent,
        (((0,), (0,)), ((), ())),
        preferred_element_type=F32,
    )
    grad = lax.psum_scatter(partial_grad, "dp", scatter_dimension=0, tiled=True)
    new_first, new_second, normalized = adam(grad, first_moment, second_moment, step_count)
    whole_steps = lax.all_gather(normalized, "dp", axis=0, tiled=True)
    out_rows = projection.shape[0] // lax.axis_size("dp")
    local_projection = lax.dynamic_slice_in_dim(
        projection, lax.axis_index("dp") * out_rows, out_rows, 0
    )
    update = jnp.dot(local_projection, whole_steps, preferred_element_type=F32).astype(BF16)
    return update, new_first, new_second


def tile_of(extent, most=512):
    return max(d for d in range(8, most + 1, 8) if extent % d == 0)


def swap(x, axis, mask):
    return lax.ppermute(x, axis, [(i, i ^ mask) for i in range(lax.axis_size(axis))])


def swap_by_core(x, masks):
    return lax.ppermute(
        x, "tensor", [(i, i ^ masks[i % 2]) for i in range(lax.axis_size("tensor"))]
    )


def row_blocks():
    replica = lax.axis_index("dp")
    return [replica ^ mask for mask in (1, 3, 0, 2)]


def lanes_of(index, size):
    return pl.ds(pl.multiple_of(index * size, size), size)


IN_VMEM = pl.BlockSpec(memory_space=pltpu.VMEM)
ANYWHERE = pl.BlockSpec(memory_space=pl.ANY)


def project(activations, projection):
    rows, width = activations.shape
    rank = projection.shape[1]
    steps = 8
    depth = width // steps

    def kernel(a_hbm, w_hbm, first, second, a_buf, w_buf, acc, sems):
        copies = []
        for k in range(steps):
            part = pl.ds(k * depth, depth)
            a_copy = pltpu.make_async_copy(a_hbm.at[:, part], a_buf.at[k], sems.at[2 * k])
            w_copy = pltpu.make_async_copy(w_hbm.at[part, :], w_buf.at[k], sems.at[2 * k + 1])
            a_copy.start()
            w_copy.start()
            copies.append((a_copy, w_copy))
        total = None
        for k, (a_copy, w_copy) in enumerate(copies):
            a_copy.wait()
            w_copy.wait()
            part = jnp.dot(a_buf[k], w_buf[k], preferred_element_type=F32)
            total = part if total is None else total + part
        acc[...] = total
        for j, block in enumerate(row_blocks()):
            out = (first, second)[j // 2]
            out[:, (j % 2) * LANES : (j % 2 + 1) * LANES] = acc[:, lanes_of(block, LANES)].astype(BF16)

    return pl.pallas_call(
        kernel,
        in_specs=[ANYWHERE, ANYWHERE],
        out_specs=[IN_VMEM, IN_VMEM],
        out_shape=[jax.ShapeDtypeStruct((rows, 2 * LANES), BF16)] * 2,
        scratch_shapes=[
            pltpu.VMEM((steps, rows, depth), BF16),
            pltpu.VMEM((steps, depth, rank), BF16),
            pltpu.VMEM((rows, rank), F32),
            pltpu.SemaphoreType.DMA((2 * steps,)),
        ],
        cost_estimate=pl.CostEstimate(
            flops=2 * rows * width * rank,
            bytes_accessed=2 * width * (rows + rank),
            transcendentals=0,
        ),
        compiler_params=pltpu.CompilerParams(vmem_limit_bytes=PROJECT_VMEM),
        name="project",
    )(activations, projection)


def load(cot_t, half):
    f_local, tokens = cot_t.shape
    f_half = f_local // 2

    def kernel(source, out, sem):
        copy = pltpu.make_async_copy(source.at[pl.ds(half * f_half, f_half), :], out, sem)
        copy.start()
        copy.wait()

    return pl.pallas_call(
        kernel,
        in_specs=[ANYWHERE],
        out_specs=IN_VMEM,
        out_shape=jax.ShapeDtypeStruct((f_half, tokens), BF16),
        scratch_shapes=[pltpu.SemaphoreType.DMA],
        cost_estimate=pl.CostEstimate(
            flops=2 * f_half * tokens, bytes_accessed=4 * f_half * tokens, transcendentals=0
        ),
        compiler_params=pltpu.CompilerParams(vmem_limit_bytes=LOAD_VMEM),
        name="load",
    )(cot_t)


def token_sum(cots, blocks, masks, total, halves):
    f_half = cots[0].shape[0]
    f_local = 2 * f_half
    rows, cols = blocks[0].shape
    n = len(blocks)
    has_total = total is not None
    tile = TOKEN_TILE if f_half % TOKEN_TILE == 0 else f_half

    def kernel(cot_0, cot_1, *refs):
        projected, rest = refs[:n], refs[n:]
        me = lax.axis_index("tensor")
        odd = me % 2
        tokens = [lanes_of(me ^ (even + odd * (uneven - even)), rows) for even, uneven in masks]
        p = jnp.concatenate([ref[...] for ref in projected], axis=0)
        for start in range(0, f_local, tile):
            here, within = pl.ds(start, tile), pl.ds(start % f_half, tile)
            cot = (cot_0, cot_1)[start // f_half]
            c = jnp.concatenate([cot[within, t] for t in tokens], axis=1)
            acc = jnp.dot(c, p, preferred_element_type=F32)
            if has_total:
                acc += rest[0][here, :]
            if halves:
                rest[-2 + start // f_half][within, :] = acc.astype(BF16)
            else:
                rest[-1][here, :] = acc

    if halves:
        out_shape = [jax.ShapeDtypeStruct((f_half, cols), BF16)] * 2
    else:
        out_shape = [jax.ShapeDtypeStruct((f_local, cols), F32)]
    out = pl.pallas_call(
        kernel,
        in_specs=[IN_VMEM] * (2 + n + has_total),
        out_specs=[IN_VMEM] * len(out_shape),
        out_shape=out_shape,
        cost_estimate=pl.CostEstimate(
            flops=2 * n * rows * cols * f_local,
            bytes_accessed=2 * n * rows * (f_local + cols) + 4 * f_local * cols,
            transcendentals=0,
        ),
        compiler_params=pltpu.CompilerParams(vmem_limit_bytes=TOKEN_VMEM),
        name="token_sum",
    )(*cots, *blocks, *([total] if has_total else []))
    return out if halves else out[0]


def pair_sum(kept, met, half):
    f_half = met.shape[0]

    def kernel(kept_ref, met_ref, out):
        mine = kept_ref[half * f_half : (half + 1) * f_half, LANES:]
        out[...] = (mine + met_ref[:, LANES:].astype(F32)).astype(BF16)

    return pl.pallas_call(
        kernel,
        in_specs=[IN_VMEM] * 2,
        out_specs=IN_VMEM,
        out_shape=jax.ShapeDtypeStruct((f_half, LANES), BF16),
        cost_estimate=pl.CostEstimate(
            flops=f_half * LANES, bytes_accessed=8 * f_half * LANES, transcendentals=0
        ),
        compiler_params=pltpu.CompilerParams(vmem_limit_bytes=SMALL_VMEM),
        name="pair_sum",
    )(kept, met)


def gradient_of(kept_ref, met_ref, across_ref, here):
    own = pl.ds(0, LANES)
    return kept_ref[here, own] + met_ref[:, own].astype(F32) + across_ref[...].astype(F32)


def moved(first, second, grad):
    return 0.9 * first + 0.1 * grad, 0.999 * second + 0.001 * grad * grad


def step_half(scales, kept, met, across, first_t, second_t, half):
    f_half = met.shape[0]

    def kernel(scale, kept_ref, met_ref, across_ref, first, second, step_ref):
        here = pl.ds(half * f_half, f_half)
        grad = gradient_of(kept_ref, met_ref, across_ref, here)
        new_first, new_second = moved(first[here, :], second[here, :], grad)
        first_hat = new_first * scale[0]
        second_hat = new_second * scale[1]
        step_ref[...] = (first_hat / (jnp.sqrt(second_hat) + 1e-08)).astype(BF16)

    return pl.pallas_call(
        kernel,
        in_specs=[pl.BlockSpec(memory_space=pltpu.SMEM)] + [IN_VMEM] * 5,
        out_specs=IN_VMEM,
        out_shape=jax.ShapeDtypeStruct((f_half, LANES), BF16),
        cost_estimate=pl.CostEstimate(
            flops=20 * f_half * LANES, bytes_accessed=18 * f_half * LANES, transcendentals=0
        ),
        compiler_params=pltpu.CompilerParams(vmem_limit_bytes=SMALL_VMEM),
        name="step_half",
    )(scales, kept, met, across, first_t, second_t)


def moments(kept, met, across, first_t, second_t):
    f_half = met[0].shape[0]

    def kernel(kept_ref, met_0, met_1, across_0, across_1, first, second, new_first, new_second):
        for half, (met_ref, across_ref) in enumerate(((met_0, across_0), (met_1, across_1))):
            here = pl.ds(half * f_half, f_half)
            grad = gradient_of(kept_ref, met_ref, across_ref, here)
            new_first[here, :], new_second[here, :] = moved(first[here, :], second[here, :], grad)

    return pl.pallas_call(
        kernel,
        in_specs=[IN_VMEM] * 7,
        out_specs=[IN_VMEM] * 2,
        out_shape=[jax.ShapeDtypeStruct(first_t.shape, F32)] * 2,
        cost_estimate=pl.CostEstimate(
            flops=20 * f_half * LANES, bytes_accessed=40 * f_half * LANES, transcendentals=0
        ),
        compiler_params=pltpu.CompilerParams(vmem_limit_bytes=SMALL_VMEM),
        name="moments",
    )(kept, *met, *across, first_t, second_t)


def apply_steps(steps, local_t, f_local, half, out):
    rows = local_t.shape[1]
    f_half = f_local // 2
    tile = tile_of(f_half)
    count = f_half // tile

    def kernel(*refs):
        w_ref = refs[4]
        out_ref, buf, sems = refs[-3:]
        blocks = row_blocks()
        w = jnp.concatenate([w_ref[lanes_of(blocks[j], LANES), :] for j in (2, 3, 0, 1)], axis=0)
        copies = []
        for k in range(count):
            x = jnp.concatenate([ref[k * tile : (k + 1) * tile, :] for ref in refs[:4]], axis=1)
            buf[k] = jnp.dot(x, w, preferred_element_type=F32).astype(BF16)
            to = out_ref.at[pl.ds(half * f_half + k * tile, tile), :]
            copies.append(pltpu.make_async_copy(buf.at[k], to, sems.at[k]))
            copies[-1].start()
        for copy in copies:
            copy.wait()

    return pl.pallas_call(
        kernel,
        in_specs=[IN_VMEM] * 5 + [ANYWHERE] * (out is not None),
        out_specs=ANYWHERE,
        out_shape=jax.ShapeDtypeStruct((f_local, rows), BF16),
        input_output_aliases={} if out is None else {5: 0},
        scratch_shapes=[pltpu.VMEM((count, tile, rows), BF16), pltpu.SemaphoreType.DMA((count,))],
        cost_estimate=pl.CostEstimate(
            flops=8 * f_half * LANES * rows,
            bytes_accessed=2 * f_half * (rows + 4 * LANES) + 8 * rows * LANES,
            transcendentals=0,
        ),
        compiler_params=pltpu.CompilerParams(vmem_limit_bytes=APPLY_VMEM),
        name="apply_steps",
    )(*steps, local_t, *([] if out is None else [out]))


MASKS = ((0, 0), (1, 1), (2, 4), (5, 3), (3, 5), (4, 2), (6, 6), (7, 7))


def stepped(activations, cotangent, projection, first_moment, second_moment, step_count):
    replica = lax.axis_index("dp")
    cot_t = cotangent.T
    f_local = cot_t.shape[0]

    first_t, second_t = first_moment.T, second_moment.T
    t_value = step_count[0].astype(F32)
    scales = 1.0 / (1.0 - jnp.power(np.array([0.9, 0.999], np.float32), t_value))
    out_rows = projection.shape[0] // lax.axis_size("dp")
    local_t = lax.dynamic_slice_in_dim(projection, replica * out_rows, out_rows, 0).T

    first, second = (2, 4), (4, 2)
    sent = project(activations, projection)
    cots = [load(cot_t, h) for h in range(2)]
    sums = []
    for s, own in zip("ab", sent):
        partner = swap(own, "tensor", 1)
        far = swap_by_core(own, first)
        far_partner = swap_by_core(partner, first)
        corner = swap_by_core(far, second)
        other_far = swap(far, "tensor", 1)
        other_far_partner = swap(far_partner, "tensor", 1)
        other_corner = swap(corner, "tensor", 1)
        near = [own, partner, far, other_far]
        total = token_sum(cots, near, MASKS[:4], None, False)
        rest = [far_partner, other_far_partner, corner, other_corner]
        sums.append(token_sum(cots, rest, MASKS[4:], total, s == "a"))
    to_send, kept = sums

    met = [swap(to_send[h], "dp", 1) for h in range(2)]
    across = [swap(pair_sum(kept, met[h], h), "dp", 2) for h in range(2)]
    steps = [step_half(scales, kept, met[h], across[h], first_t, second_t, h) for h in range(2)]
    new_first, new_second = moments(kept, met, across, first_t, second_t)
    update = None
    for h in range(2):
        step_2 = swap(steps[h], "dp", 2)
        step_1 = swap(steps[h], "dp", 1)
        step_3 = swap(step_2, "dp", 1)
        update = apply_steps([steps[h], step_2, step_1, step_3], local_t, f_local, h, update)
    return update.T, new_first.T, new_second.T


def solution(mesh):
    in_specs = (
        P(("dp", "tensor"), None),
        P("dp", "tensor"),
        P(),
        P("dp", "tensor"),
        P("dp", "tensor"),
        P(),
    )
    out_specs = (P("dp", "tensor"), P("dp", "tensor"), P("dp", "tensor"))
    exchanges = mesh.shape["dp"] == 4 and mesh.shape["tensor"] == 8

    def per_device(activations, cotangent, projection, first_moment, second_moment, step_count):
        fits = (
            exchanges
            and first_moment.shape[0] == LANES
            and cotangent.shape[1] % 16 == 0
            and activations.shape[0] % LANES == 0
        )
        if not fits:
            return plain(
                activations, cotangent, projection, first_moment, second_moment, step_count
            )
        return stepped(activations, cotangent, projection, first_moment, second_moment, step_count)

    return jax.shard_map(
        per_device, mesh=mesh, in_specs=in_specs, out_specs=out_specs, check_vma=False
    )
```

time: 169 us -> 96.6 us (0.57)
  waiting for transfers between devices: 129 us -> 35.1 us
  Pallas kernels: 0 us -> 26.7 us
  starting transfers between devices: 0.12 us -> 25.2 us
  matrix products: 22.6 us -> 0 us
  between operations: 14.5 us -> 1.52 us
  local copies, waits for them, and re-layouts: 0.01 us -> 7.7 us
  other arithmetic: 2.55 us -> 0.02 us
    all_gather x2 -> x0, waiting for transfers between devices: 74.3 us -> none  [the longest x1 39.4 us: per_device(): lax.all_gather(projected, 'tensor', axis=0, tiled=True)]
    reduce_scatter x1 -> x0, waiting for transfers between devices: 54.7 us -> none  [per_device(): grad = lax.psum_scatter(partial_grad, 'dp', scatter_dimension=0, tiled=True)]
    ppermute x0 -> x24, waiting for transfers between devices: none -> 35.1 us  [the longest x18 28.7 us: swap(): lax.ppermute(x, axis, [(i, i ^ mask) for i in range(lax.axis_size(axis))])]
    pallas_call x0 -> x14, Pallas kernels: none -> 26.7 us  [the longest x4 6.64 us: token_sum(): pl.pallas_call(kernel, in_specs=[IN_VMEM] * (2 + n + has_total), out_spec...]
    ppermute x0 -> x24, starting transfers between devices: none -> 25.2 us  [the longest x18 13.7 us: swap(): lax.ppermute(x, axis, [(i, i ^ mask) for i in range(lax.axis_size(axis))])]
    dot_general x3 -> x0, matrix products: 22.6 us -> none  [the longest x1 11.1 us: per_device(): lax.dot_general(lax.all_gather(projected, 'tensor', axis=0, tiled=True),...]
    unnamed x4 -> x21, local copies, waits for them, and re-layouts: 0.01 us -> 5.44 us
    convert_element_type x1 -> x0, other arithmetic: 2.55 us -> none  [per_device(): (first_hat / (jnp.sqrt(second_hat) + 1e-08)).astype(jnp.bfloat16)]
  transfers between devices with their start and end apart: 3 -> 24, of which waited for: 3 -> 8; matrix products, arithmetic and copies ran while one was open for 0% -> 4% of each run, Pallas kernels for 0% -> 20%
where the time goes in v1:
time: 96.6 us; the launch traced here: 96.2 us
  waiting for transfers between devices  35.1 us (36%)
  Pallas kernels  26.7 us (28%)
  starting transfers between devices  25.2 us (26%)
  local copies, waits for them, and re-layouts  7.7 us (8%)
  between operations  1.52 us (2%)
    ppermute x18, waiting for transfers between devices, swap(): lax.ppermute(x, axis, [(i, i ^ mask) for i in range(lax.axis_size(axis))])  28.7 us
    ppermute x18, starting transfers between devices, swap(): lax.ppermute(x, axis, [(i, i ^ mask) for i in range(lax.axis_size(axis))])  13.7 us
    ppermute x6, starting transfers between devices, swap_by_core(): lax.ppermute(x, 'tensor', [(i, i ^ masks[i % 2]) for i in range(lax.axis_...  11.5 us
    pallas_call x4, Pallas kernels, token_sum(): pl.pallas_call(kernel, in_specs=[IN_VMEM] * (2 + n + has_total), out_spec...  6.64 us
    ppermute x6, waiting for transfers between devices, swap_by_core(): lax.ppermute(x, 'tensor', [(i, i ^ masks[i % 2]) for i in range(lax.axis_...  6.43 us
    pallas_call x2, Pallas kernels, apply_steps(): pl.pallas_call(kernel, in_specs=[IN_VMEM] * 5 + [ANYWHERE] * (out is not...  5.94 us
    unnamed x21, local copies, waits for them, and re-layouts  5.44 us
    pallas_call x2, Pallas kernels, load(): pl.pallas_call(kernel, in_specs=[ANYWHERE], out_specs=IN_VMEM, out_shape=...  5.22 us
  transfers between devices with their start and end apart: 24, of which 8 were waited for; matrix products, arithmetic and copies ran while one was open for 4% of the time, Pallas kernels for 20%

profile of v1, /device:TPU:0, one launch (start us, length us, event | category | flops | bytes accessed | tf_op | source)
XLA Modules:
  0.0 96.2 jit_solution(12763840582046089894)
XLA Ops:
  0.6 4.5 %project.1 = (bf16[512,256]{1,0:T(8,128)(2,1)S(1)}, bf16[512,256]{1,0:T(8,128)(2,1)S(1)}) custom-call(bf16[512,4096]{1,0:T(8,128)(2,1)} %a_hbm.1, bf16[4096,512]{1,0:T(8,128)(2,1)} %w_hbm.1), custom_call_target="tpu_custom_call" | custom-call | flops 2147483648 | bytes 8388608 | tf_op jit(solution)/shard_map/project/pallas_call | solution.py:103
  5.1 3.0 %collective-permute-start.10 = (bf16[512,256]{1,0:T(8,128)(2,1)S(1)}, bf16[512,256]{1,0:T(8,128)(2,1)S(1)}, u32[]{:S(2)}, u32[]{:S(2)}) collective-permute-start(bf16[512,256]{1,0:T(8,128)(2,1)S(1)} %get-tuple-element.10.refs_0_), channel_id=1, source_target_pairs={{0,2},{1,5},{2,0},{3,7},{4,6},{5,1},{6,4},{7,3},{8,10},{9,13},{10,... | collective-permute-start | bytes 786440 | tf_op jit(solution)/shard_map/ppermute | solution.py:59
  8.2 0.0 collective-permute-start.7
  8.2 1.1 %collective-permute-start.3 = (bf16[512,256]{1,0:T(8,128)(2,1)S(1)}, bf16[512,256]{1,0:T(8,128)(2,1)S(1)}, u32[]{:S(2)}, u32[]{:S(2)}) collective-permute-start(bf16[512,256]{1,0:T(8,128)(2,1)S(1)} %get-tuple-element.9.refs_0_), channel_id=1, source_target_pairs={{0,2},{1,5},{2,0},{3,7},{4,6},{5,1},{6,4},{7,3},{8,10},{9,13},{10,... | collective-permute-start | bytes 786440 | tf_op jit(solution)/shard_map/ppermute | solution.py:59
  9.2 0.7 collective-permute-start
  9.9 2.6 %collective-permute-done.10.refs_2_ = bf16[512,256]{1,0:T(8,128)(2,1)S(1)} collective-permute-done((bf16[512,256]{1,0:T(8,128)(2,1)S(1)}, bf16[512,256]{1,0:T(8,128)(2,1)S(1)}, u32[]{:S(2)}, u32[]{:S(2)}) %collective-permute-start.10) | collective-permute-done | bytes 262176 | tf_op jit(solution)/shard_map/ppermute | solution.py:59
  12.5 2.0 %collective-permute-start.11 = (bf16[512,256]{1,0:T(8,128)(2,1)S(1)}, bf16[512,256]{1,0:T(8,128)(2,1)S(1)}, u32[]{:S(2)}, u32[]{:S(2)}) collective-permute-start(bf16[512,256]{1,0:T(8,128)(2,1)S(1)} %collective-permute-done.10.refs_2_), channel_id=1, source_target_pairs={{0,4},{1,3},{2,6},{3,1},{4,0},{5,7},{6,2},{7,5},{8,12},{9,11},{10,... | collective-permute-start | bytes 786440 | tf_op jit(solution)/shard_map/ppermute | solution.py:59
  14.6 0.0 collective-permute-done.7.refs_1_
  14.6 1.5 %collective-permute-start.8 = (bf16[512,256]{1,0:T(8,128)(2,1)S(1)}, bf16[512,256]{1,0:T(8,128)(2,1)S(1)}, u32[]{:S(2)}, u32[]{:S(2)}) collective-permute-start(bf16[512,256]{1,0:T(8,128)(2,1)S(1)} %collective-permute-done.7.refs_1_), channel_id=1, source_target_pairs={{0,2},{1,5},{2,0},{3,7},{4,6},{5,1},{6,4},{7,3},{8,10},{9,13},{10,... | collective-permute-start | bytes 786440 | tf_op jit(solution)/shard_map/ppermute | solution.py:59
  16.0 0.2 collective-permute-done.3.refs_2_
  16.2 2.4 %collective-permute-start.4 = (bf16[512,256]{1,0:T(8,128)(2,1)S(1)}, bf16[512,256]{1,0:T(8,128)(2,1)S(1)}, u32[]{:S(2)}, u32[]{:S(2)}) collective-permute-start(bf16[512,256]{1,0:T(8,128)(2,1)S(1)} %collective-permute-done.3.refs_2_), channel_id=1, source_target_pairs={{0,4},{1,3},{2,6},{3,1},{4,0},{5,7},{6,2},{7,5},{8,12},{9,11},{10,... | collective-permute-start | bytes 786440 | tf_op jit(solution)/shard_map/ppermute | solution.py:59
  18.6 0.0 collective-permute-done.refs_1_
  18.6 1.5 %collective-permute-start.1 = (bf16[512,256]{1,0:T(8,128)(2,1)S(1)}, bf16[512,256]{1,0:T(8,128)(2,1)S(1)}, u32[]{:S(2)}, u32[]{:S(2)}) collective-permute-start(bf16[512,256]{1,0:T(8,128)(2,1)S(1)} %collective-permute-done.refs_1_), channel_id=1, source_target_pairs={{0,2},{1,5},{2,0},{3,7},{4,6},{5,1},{6,4},{7,3},{8,10},{9,13},{10,... | collective-permute-start | bytes 786440 | tf_op jit(solution)/shard_map/ppermute | solution.py:59
  20.1 0.0 collective-permute-start.13
  20.1 1.6 %collective-permute-done.11.refs_2_ = bf16[512,256]{1,0:T(8,128)(2,1)S(1)} collective-permute-done((bf16[512,256]{1,0:T(8,128)(2,1)S(1)}, bf16[512,256]{1,0:T(8,128)(2,1)S(1)}, u32[]{:S(2)}, u32[]{:S(2)}) %collective-permute-start.11) | collective-permute-done | bytes 262176 | tf_op jit(solution)/shard_map/ppermute | solution.py:59
  21.7 2.0 %collective-permute-done.8.refs_0_ = bf16[512,256]{1,0:T(8,128)(2,1)S(1)} collective-permute-done((bf16[512,256]{1,0:T(8,128)(2,1)S(1)}, bf16[512,256]{1,0:T(8,128)(2,1)S(1)}, u32[]{:S(2)}, u32[]{:S(2)}) %collective-permute-start.8) | collective-permute-done | bytes 262176 | tf_op jit(solution)/shard_map/ppermute | solution.py:59
  23.7 0.0 collective-permute-start.9
  23.7 2.6 %load.2.cot_0 = bf16[688,4096]{1,0:T(8,128)(2,1)S(1)} custom-call(bf16[1376,4096]{1,0:T(8,128)(2,1)} %bitcast.16), custom_call_target="tpu_custom_call" | custom-call | flops 5636096 | bytes 11272192 | tf_op jit(solution)/shard_map/load/pallas_call | solution.py:133
  26.4 2.6 %load.3.cot_1 = bf16[688,4096]{1,0:T(8,128)(2,1)S(1)} custom-call(bf16[1376,4096]{1,0:T(8,128)(2,1)} %bitcast.17), custom_call_target="tpu_custom_call" | custom-call | flops 5636096 | bytes 11272192 | tf_op jit(solution)/shard_map/load/pallas_call | solution.py:133
  29.0 0.6 collective-permute-start.6
  29.6 0.0 collective-permute-done.1.refs_0_
  29.6 0.1 collective-permute-start.5
  29.6 0.0 collective-permute-done.13.refs_3_
  29.6 0.4 collective-permute-start.2
  30.1 1.6 %token_sum.6.refs_4_ = f32[1376,256]{1,0:T(8,128)S(1)} custom-call(bf16[688,4096]{1,0:T(8,128)(2,1)S(1)} %load.2.cot_0, bf16[688,4096]{1,0:T(8,128)(2,1)S(1)} %load.3.cot_1, bf16[512,256]{1,0:T(8,128)(2,1)S(1)} %get-tuple-element.10.refs_0_, bf16[512,256]{1,0:T(8,128)(2,1)S(1)} %collective-permute-done.7.refs_1_, ...), custom_call_target="tpu_custom_call" | custom-call | flops 1442840576 | bytes 8093696 | tf_op jit(solution)/shard_map/token_sum/pallas_call | solution.py:177
  31.7 0.0 collective-permute-done.12.refs_3_
  31.7 1.7 %token_sum.7 = (bf16[688,256]{1,0:T(8,128)(2,1)S(1)}, bf16[688,256]{1,0:T(8,128)(2,1)S(1)}) custom-call(bf16[688,4096]{1,0:T(8,128)(2,1)S(1)} %load.2.cot_0, bf16[688,4096]{1,0:T(8,128)(2,1)S(1)} %load.3.cot_1, bf16[512,256]{1,0:T(8,128)(2,1)S(1)} %collective-permute-done.8.refs_0_, bf16[512,256]{1,0:T(8,128)(2,1)S(1)} %collective-permute-done.9.refs_1_, ...), custom_call_target="tpu_custom_call" | custom-call | flops 1442840576 | bytes 8093696 | tf_op jit(solution)/shard_map/token_sum/pallas_call | solution.py:177
  33.4 1.7 %collective-permute-start.19 = (bf16[688,256]{1,0:T(8,128)(2,1)S(1)}, bf16[688,256]{1,0:T(8,128)(2,1)S(1)}, u32[]{:S(2)}, u32[]{:S(2)}) collective-permute-start(bf16[688,256]{1,0:T(8,128)(2,1)S(1)} %get-tuple-element.12), channel_id=1, source_target_pairs={{0,8},{8,0},{16,24},{24,16},{1,9},{9,1},{17,25},{25,17},{2,10},{10... | collective-permute-start | bytes 1056776 | tf_op jit(solution)/shard_map/ppermute | solution.py:55
  35.1 0.4 collective-permute-start.14
  36.2 1.6 %token_sum.4.refs_4_ = f32[1376,256]{1,0:T(8,128)S(1)} custom-call(bf16[688,4096]{1,0:T(8,128)(2,1)S(1)} %load.2.cot_0, bf16[688,4096]{1,0:T(8,128)(2,1)S(1)} %load.3.cot_1, bf16[512,256]{1,0:T(8,128)(2,1)S(1)} %get-tuple-element.9.refs_0_, bf16[512,256]{1,0:T(8,128)(2,1)S(1)} %collective-permute-done.refs_1_, ...), custom_call_target="tpu_custom_call" | custom-call | flops 1442840576 | bytes 8093696 | tf_op jit(solution)/shard_map/token_sum/pallas_call | solution.py:177
  37.8 0.0 copy-start.9
  37.9 0.0 collective-permute-done.5.refs_3_
  37.9 0.0 collective-permute-done.2.refs_1_
  37.9 1.7 %token_sum.5.kept_ref = f32[1376,256]{1,0:T(8,128)S(1)} custom-call(bf16[688,4096]{1,0:T(8,128)(2,1)S(1)} %load.2.cot_0, bf16[688,4096]{1,0:T(8,128)(2,1)S(1)} %load.3.cot_1, bf16[512,256]{1,0:T(8,128)(2,1)S(1)} %collective-permute-done.1.refs_0_, bf16[512,256]{1,0:T(8,128)(2,1)S(1)} %collective-permute-done.2.refs_1_, ...), custom_call_target="tpu_custom_call" | custom-call | flops 1442840576 | bytes 8093696 | tf_op jit(solution)/shard_map/token_sum/pallas_call | solution.py:177
  39.5 0.0 copy-start
  39.6 0.0 copy-start.1
  39.6 5.0 %collective-permute-done.19.met_ref.met_0 = bf16[688,256]{1,0:T(8,128)(2,1)S(1)} collective-permute-done((bf16[688,256]{1,0:T(8,128)(2,1)S(1)}, bf16[688,256]{1,0:T(8,128)(2,1)S(1)}, u32[]{:S(2)}, u32[]{:S(2)}) %collective-permute-start.19) | collective-permute-done | bytes 352288 | tf_op jit(solution)/shard_map/ppermute | solution.py:55
  44.6 2.7 %collective-permute-start.20 = (bf16[688,128]{1,0:T(8,128)(2,1)S(1)}, bf16[688,128]{1,0:T(8,128)(2,1)S(1)}, u32[]{:S(2)}, u32[]{:S(2)}) collective-permute-start(bf16[688,128]{1,0:T(8,128)(2,1)S(1)} %pair_sum.3), channel_id=1, source_target_pairs={{0,16},{8,24},{16,0},{24,8},{1,17},{9,25},{17,1},{25,9},{2,18},{10... | collective-permute-start | bytes 528392 | tf_op jit(solution)/shard_map/ppermute | solution.py:55
  47.3 7.7 %collective-permute-done.14.met_ref.met_1 = bf16[688,256]{1,0:T(8,128)(2,1)S(1)} collective-permute-done((bf16[688,256]{1,0:T(8,128)(2,1)S(1)}, bf16[688,256]{1,0:T(8,128)(2,1)S(1)}, u32[]{:S(2)}, u32[]{:S(2)}) %collective-permute-start.14) | collective-permute-done | bytes 352288 | tf_op jit(solution)/shard_map/ppermute | solution.py:55
  55.1 1.7 %collective-permute-start.15 = (bf16[688,128]{1,0:T(8,128)(2,1)S(1)}, bf16[688,128]{1,0:T(8,128)(2,1)S(1)}, u32[]{:S(2)}, u32[]{:S(2)}) collective-permute-start(bf16[688,128]{1,0:T(8,128)(2,1)S(1)} %pair_sum.2), channel_id=1, source_target_pairs={{0,16},{8,24},{16,0},{24,8},{1,17},{9,25},{17,1},{25,9},{2,18},{10... | collective-permute-start | bytes 528392 | tf_op jit(solution)/shard_map/ppermute | solution.py:55
  56.8 0.0 collective-permute-done.20.across_ref.across_0
  56.9 0.0 copy-start.5
  56.9 1.5 %step_half.3.refs_0_ = bf16[688,128]{1,0:T(8,128)(2,1)} custom-call(f32[2]{0:T(128)S(1)} %subtract_divide_fusion.scale, f32[1376,256]{1,0:T(8,128)S(1)} %token_sum.5.kept_ref, bf16[688,256]{1,0:T(8,128)(2,1)S(1)} %collective-permute-done.19.met_ref.met_0, bf16[688,128]{1,0:T(8,128)(2,1)S(1)} %collective-permute-done.20.across_ref.across_0, ...), custom_call_target="tpu_custom_call" | custom-call | flops 1761280 | bytes 1585152 | tf_op jit(solution)/shard_map/step_half/pallas_call | solution.py:233
  58.4 1.2 %collective-permute-start.21 = (bf16[688,128]{1,0:T(8,128)(2,1)}, bf16[688,128]{1,0:T(8,128)(2,1)}, u32[]{:S(2)}, u32[]{:S(2)}) collective-permute-start(bf16[688,128]{1,0:T(8,128)(2,1)} %step_half.3.refs_0_), channel_id=1, source_target_pairs={{0,16},{8,24},{16,0},{24,8},{1,17},{9,25},{17,1},{25,9},{2,18},{10... | collective-permute-start | bytes 528392 | tf_op jit(solution)/shard_map/ppermute | solution.py:55
  59.6 10.6 %collective-permute-done.15.across_ref.across_1 = bf16[688,128]{1,0:T(8,128)(2,1)S(1)} collective-permute-done((bf16[688,128]{1,0:T(8,128)(2,1)S(1)}, bf16[688,128]{1,0:T(8,128)(2,1)S(1)}, u32[]{:S(2)}, u32[]{:S(2)}) %collective-permute-start.15) | collective-permute-done | bytes 176160 | tf_op jit(solution)/shard_map/ppermute | solution.py:55
  70.2 1.5 %step_half.2.refs_0_ = bf16[688,128]{1,0:T(8,128)(2,1)} custom-call(f32[2]{0:T(128)S(1)} %subtract_divide_fusion.scale, f32[1376,256]{1,0:T(8,128)S(1)} %token_sum.5.kept_ref, bf16[688,256]{1,0:T(8,128)(2,1)S(1)} %collective-permute-done.14.met_ref.met_1, bf16[688,128]{1,0:T(8,128)(2,1)S(1)} %collective-permute-done.15.across_ref.across_1, ...), custom_call_target="tpu_custom_call" | custom-call | flops 1761280 | bytes 1585152 | tf_op jit(solution)/shard_map/step_half/pallas_call | solution.py:233
  71.7 2.2 %collective-permute-start.22 = (bf16[688,128]{1,0:T(8,128)(2,1)}, bf16[688,128]{1,0:T(8,128)(2,1)}, u32[]{:S(2)}, u32[]{:S(2)}) collective-permute-start(bf16[688,128]{1,0:T(8,128)(2,1)} %step_half.3.refs_0_), channel_id=1, source_target_pairs={{0,8},{8,0},{16,24},{24,16},{1,9},{9,1},{17,25},{25,17},{2,10},{10... | collective-permute-start | bytes 528392 | tf_op jit(solution)/shard_map/ppermute | solution.py:55
  73.9 0.9 collective-permute-start.23
  74.8 1.1 %collective-permute-start.17 = (bf16[688,128]{1,0:T(8,128)(2,1)}, bf16[688,128]{1,0:T(8,128)(2,1)}, u32[]{:S(2)}, u32[]{:S(2)}) collective-permute-start(bf16[688,128]{1,0:T(8,128)(2,1)} %step_half.2.refs_0_), channel_id=1, source_target_pairs={{0,8},{8,0},{16,24},{24,16},{1,9},{9,1},{17,25},{25,17},{2,10},{10... | collective-permute-start | bytes 528392 | tf_op jit(solution)/shard_map/ppermute | solution.py:55
  75.9 5.3 %collective-permute-done.16.refs_1_ = bf16[688,128]{1,0:T(8,128)(2,1)} collective-permute-done((bf16[688,128]{1,0:T(8,128)(2,1)}, bf16[688,128]{1,0:T(8,128)(2,1)}, u32[]{:S(2)}, u32[]{:S(2)}) %collective-permute-start.16) | collective-permute-done | bytes 176160 | tf_op jit(solution)/shard_map/ppermute | solution.py:55
  81.2 0.0 collective-permute-start.18
  81.2 2.3 %constant_dynamic-slice_fusion = bf16[1024,512]{1,0:T(8,128)(2,1)} fusion(bf16[4096,512]{1,0:T(8,128)(2,1)} %w_hbm.1, s32[]{:T(128)S(6)} %select_n.3), kind=kLoop, calls=%fused_computation.1 | loop fusion | bytes 2097156 | tf_op jit(solution)/shard_map/dynamic_slice | solution.py:318
  83.5 1.5 %copy.12 = bf16[1024,512]{0,1:T(8,128)(2,1)S(1)} copy(bf16[1024,512]{1,0:T(8,128)(2,1)} %constant_dynamic-slice_fusion) | data formatting | bytes 2097152
  85.0 0.0 copy-start.2
  85.0 1.1 %copy-done.2 = f32[128,1376]{0,1:T(8,128)S(1)} copy-done((f32[128,1376]{0,1:T(8,128)S(1)}, f32[128,1376]{0,1:T(8,128)}, u32[]{:S(2)}) %copy-start.2) | copy-done | bytes 704536
  86.1 1.0 %copy-done.4 = bf16[688,256]{1,0:T(8,128)(2,1)S(1)} copy-done((bf16[688,256]{1,0:T(8,128)(2,1)S(1)}, bf16[688,256]{1,0:T(8,128)(2,1)}, u32[]{:S(2)}) %copy-start.4) | copy-done | bytes 352280
  87.1 0.9 copy-done.6
  88.0 0.9 copy-done.8
  88.9 1.3 %moments.1 = (f32[1376,128]{1,0:T(8,128)}, f32[1376,128]{1,0:T(8,128)}) custom-call(f32[1376,256]{1,0:T(8,128)S(1)} %token_sum.5.kept_ref, bf16[688,256]{1,0:T(8,128)(2,1)S(1)} %collective-permute-done.19.met_ref.met_0, bf16[688,256]{1,0:T(8,128)(2,1)S(1)} %copy-done.4, bf16[688,128]{1,0:T(8,128)(2,1)S(1)} %copy-done.6, bf16[688,128]{1,0:T(8,128)(2,1)S(1)} %copy-done.8, ...), custom_call_target="tpu_custom_call" | custom-call | flops 1761280 | bytes 3522560 | tf_op jit(solution)/shard_map/moments/pallas_call | solution.py:255
  90.2 0.0 collective-permute-done.22.refs_2_
  90.2 0.0 collective-permute-done.23.refs_3_
  90.2 3.0 %apply_steps.2.refs_5_ = bf16[1376,1024]{1,0:T(8,128)(2,1)} custom-call(bf16[688,128]{1,0:T(8,128)(2,1)} %step_half.3.refs_0_, bf16[688,128]{1,0:T(8,128)(2,1)} %collective-permute-done.21.refs_1_, bf16[688,128]{1,0:T(8,128)(2,1)} %collective-permute-done.22.refs_2_, bf16[688,128]{1,0:T(8,128)(2,1)} %collective-permute-done.23.refs_3_, ...), custom_call_target="tpu_custom_call" | custom-call | flops 721420288 | bytes 3162112 | tf_op jit(solution)/shard_map/apply_steps/pallas_call | solution.py:289
  93.2 0.0 collective-permute-done.17.refs_2_
  93.2 3.0 %apply_steps.3 = bf16[1376,1024]{1,0:T(8,128)(2,1)} custom-call(bf16[688,128]{1,0:T(8,128)(2,1)} %step_half.2.refs_0_, bf16[688,128]{1,0:T(8,128)(2,1)} %collective-permute-done.16.refs_1_, bf16[688,128]{1,0:T(8,128)(2,1)} %collective-permute-done.17.refs_2_, bf16[688,128]{1,0:T(8,128)(2,1)} %collective-permute-done.18.refs_3_, ...), custom_call_target="tpu_custom_call", output_to_operand_aliasing={{}: (5, {})} | custom-call | flops 721420288 | bytes 3162112 | tf_op jit(solution)/shard_map/apply_steps/pallas_call | solution.py:289
  (21 shorter events, 0.1 us)
Async XLA Ops:
  5.1 7.4 %collective-permute-start.10 = (bf16[512,256]{1,0:T(8,128)(2,1)S(1)}, bf16[512,256]{1,0:T(8,128)(2,1)S(1)}, u32[]{:S(2)}, u32[]{:S(2)}) collective-permute-start(bf16[512,256]{1,0:T(8,128)(2,1)S(1)} %get-tuple-element.10.refs_0_), channel_id=1, source_target_pairs={{0,2},{1,5},{2,0},{3,7},{4,6},{5,1},{6,4},{7,3},{8,10},{9,13},{10,... | collective-permute-start | bytes 786440 | tf_op jit(solution)/shard_map/ppermute | solution.py:59
  8.2 6.4 %collective-permute-start.7 = (bf16[512,256]{1,0:T(8,128)(2,1)S(1)}, bf16[512,256]{1,0:T(8,128)(2,1)S(1)}, u32[]{:S(2)}, u32[]{:S(2)}) collective-permute-start(bf16[512,256]{1,0:T(8,128)(2,1)S(1)} %get-tuple-element.10.refs_0_), channel_id=1, source_target_pairs={{0,1},{1,0},{2,3},{3,2},{4,5},{5,4},{6,7},{7,6},{8,9},{9,8},{10,11... | collective-permute-start | bytes 786440 | tf_op jit(solution)/shard_map/ppermute | solution.py:55
  8.2 8.1 %collective-permute-start.3 = (bf16[512,256]{1,0:T(8,128)(2,1)S(1)}, bf16[512,256]{1,0:T(8,128)(2,1)S(1)}, u32[]{:S(2)}, u32[]{:S(2)}) collective-permute-start(bf16[512,256]{1,0:T(8,128)(2,1)S(1)} %get-tuple-element.9.refs_0_), channel_id=1, source_target_pairs={{0,2},{1,5},{2,0},{3,7},{4,6},{5,1},{6,4},{7,3},{8,10},{9,13},{10,... | collective-permute-start | bytes 786440 | tf_op jit(solution)/shard_map/ppermute | solution.py:59
  9.2 9.4 %collective-permute-start = (bf16[512,256]{1,0:T(8,128)(2,1)S(1)}, bf16[512,256]{1,0:T(8,128)(2,1)S(1)}, u32[]{:S(2)}, u32[]{:S(2)}) collective-permute-start(bf16[512,256]{1,0:T(8,128)(2,1)S(1)} %get-tuple-element.9.refs_0_), channel_id=1, source_target_pairs={{0,1},{1,0},{2,3},{3,2},{4,5},{5,4},{6,7},{7,6},{8,9},{9,8},{10,11... | collective-permute-start | bytes 786440 | tf_op jit(solution)/shard_map/ppermute | solution.py:55
  12.5 9.2 %collective-permute-start.11 = (bf16[512,256]{1,0:T(8,128)(2,1)S(1)}, bf16[512,256]{1,0:T(8,128)(2,1)S(1)}, u32[]{:S(2)}, u32[]{:S(2)}) collective-permute-start(bf16[512,256]{1,0:T(8,128)(2,1)S(1)} %collective-permute-done.10.refs_2_), channel_id=1, source_target_pairs={{0,4},{1,3},{2,6},{3,1},{4,0},{5,7},{6,2},{7,5},{8,12},{9,11},{10,... | collective-permute-start | bytes 786440 | tf_op jit(solution)/shard_map/ppermute | solution.py:59
  14.6 9.2 %collective-permute-start.8 = (bf16[512,256]{1,0:T(8,128)(2,1)S(1)}, bf16[512,256]{1,0:T(8,128)(2,1)S(1)}, u32[]{:S(2)}, u32[]{:S(2)}) collective-permute-start(bf16[512,256]{1,0:T(8,128)(2,1)S(1)} %collective-permute-done.7.refs_1_), channel_id=1, source_target_pairs={{0,2},{1,5},{2,0},{3,7},{4,6},{5,1},{6,4},{7,3},{8,10},{9,13},{10,... | collective-permute-start | bytes 786440 | tf_op jit(solution)/shard_map/ppermute | solution.py:59
  16.2 12.7 %collective-permute-start.4 = (bf16[512,256]{1,0:T(8,128)(2,1)S(1)}, bf16[512,256]{1,0:T(8,128)(2,1)S(1)}, u32[]{:S(2)}, u32[]{:S(2)}) collective-permute-start(bf16[512,256]{1,0:T(8,128)(2,1)S(1)} %collective-permute-done.3.refs_2_), channel_id=1, source_target_pairs={{0,4},{1,3},{2,6},{3,1},{4,0},{5,7},{6,2},{7,5},{8,12},{9,11},{10,... | collective-permute-start | bytes 786440 | tf_op jit(solution)/shard_map/ppermute | solution.py:59
  18.6 11.0 %collective-permute-start.1 = (bf16[512,256]{1,0:T(8,128)(2,1)S(1)}, bf16[512,256]{1,0:T(8,128)(2,1)S(1)}, u32[]{:S(2)}, u32[]{:S(2)}) collective-permute-start(bf16[512,256]{1,0:T(8,128)(2,1)S(1)} %collective-permute-done.refs_1_), channel_id=1, source_target_pairs={{0,2},{1,5},{2,0},{3,7},{4,6},{5,1},{6,4},{7,3},{8,10},{9,13},{10,... | collective-permute-start | bytes 786440 | tf_op jit(solution)/shard_map/ppermute | solution.py:59
  20.1 9.6 %collective-permute-start.13 = (bf16[512,256]{1,0:T(8,128)(2,1)S(1)}, bf16[512,256]{1,0:T(8,128)(2,1)S(1)}, u32[]{:S(2)}, u32[]{:S(2)}) collective-permute-start(bf16[512,256]{1,0:T(8,128)(2,1)S(1)} %collective-permute-done.10.refs_2_), channel_id=1, source_target_pairs={{0,1},{1,0},{2,3},{3,2},{4,5},{5,4},{6,7},{7,6},{8,9},{9,8},{10,11... | collective-permute-start | bytes 786440 | tf_op jit(solution)/shard_map/ppermute | solution.py:55
  21.7 10.0 %collective-permute-start.12 = (bf16[512,256]{1,0:T(8,128)(2,1)S(1)}, bf16[512,256]{1,0:T(8,128)(2,1)S(1)}, u32[]{:S(2)}, u32[]{:S(2)}) collective-permute-start(bf16[512,256]{1,0:T(8,128)(2,1)S(1)} %collective-permute-done.11.refs_2_), channel_id=1, source_target_pairs={{0,1},{1,0},{2,3},{3,2},{4,5},{5,4},{6,7},{7,6},{8,9},{9,8},{10,11... | collective-permute-start | bytes 786440 | tf_op jit(solution)/shard_map/ppermute | solution.py:55
  23.7 8.0 %collective-permute-start.9 = (bf16[512,256]{1,0:T(8,128)(2,1)S(1)}, bf16[512,256]{1,0:T(8,128)(2,1)S(1)}, u32[]{:S(2)}, u32[]{:S(2)}) collective-permute-start(bf16[512,256]{1,0:T(8,128)(2,1)S(1)} %collective-permute-done.8.refs_0_), channel_id=1, source_target_pairs={{0,1},{1,0},{2,3},{3,2},{4,5},{5,4},{6,7},{7,6},{8,9},{9,8},{10,11... | collective-permute-start | bytes 786440 | tf_op jit(solution)/shard_map/ppermute | solution.py:55
  29.0 7.2 %collective-permute-start.6 = (bf16[512,256]{1,0:T(8,128)(2,1)S(1)}, bf16[512,256]{1,0:T(8,128)(2,1)S(1)}, u32[]{:S(2)}, u32[]{:S(2)}) collective-permute-start(bf16[512,256]{1,0:T(8,128)(2,1)S(1)} %collective-permute-done.3.refs_2_), channel_id=1, source_target_pairs={{0,1},{1,0},{2,3},{3,2},{4,5},{5,4},{6,7},{7,6},{8,9},{9,8},{10,11... | collective-permute-start | bytes 786440 | tf_op jit(solution)/shard_map/ppermute | solution.py:55
  29.6 8.3 %collective-permute-start.5 = (bf16[512,256]{1,0:T(8,128)(2,1)S(1)}, bf16[512,256]{1,0:T(8,128)(2,1)S(1)}, u32[]{:S(2)}, u32[]{:S(2)}) collective-permute-start(bf16[512,256]{1,0:T(8,128)(2,1)S(1)} %collective-permute-done.4.refs_2_), channel_id=1, source_target_pairs={{0,1},{1,0},{2,3},{3,2},{4,5},{5,4},{6,7},{7,6},{8,9},{9,8},{10,11... | collective-permute-start | bytes 786440 | tf_op jit(solution)/shard_map/ppermute | solution.py:55
  29.6 8.2 %collective-permute-start.2 = (bf16[512,256]{1,0:T(8,128)(2,1)S(1)}, bf16[512,256]{1,0:T(8,128)(2,1)S(1)}, u32[]{:S(2)}, u32[]{:S(2)}) collective-permute-start(bf16[512,256]{1,0:T(8,128)(2,1)S(1)} %collective-permute-done.1.refs_0_), channel_id=1, source_target_pairs={{0,1},{1,0},{2,3},{3,2},{4,5},{5,4},{6,7},{7,6},{8,9},{9,8},{10,11... | collective-permute-start | bytes 786440 | tf_op jit(solution)/shard_map/ppermute | solution.py:55
  33.4 11.2 %collective-permute-start.19 = (bf16[688,256]{1,0:T(8,128)(2,1)S(1)}, bf16[688,256]{1,0:T(8,128)(2,1)S(1)}, u32[]{:S(2)}, u32[]{:S(2)}) collective-permute-start(bf16[688,256]{1,0:T(8,128)(2,1)S(1)} %get-tuple-element.12), channel_id=1, source_target_pairs={{0,8},{8,0},{16,24},{24,16},{1,9},{9,1},{17,25},{25,17},{2,10},{10... | collective-permute-start | bytes 1056776 | tf_op jit(solution)/shard_map/ppermute | solution.py:55
  35.1 19.9 %collective-permute-start.14 = (bf16[688,256]{1,0:T(8,128)(2,1)S(1)}, bf16[688,256]{1,0:T(8,128)(2,1)S(1)}, u32[]{:S(2)}, u32[]{:S(2)}) collective-permute-start(bf16[688,256]{1,0:T(8,128)(2,1)S(1)} %get-tuple-element.11), channel_id=1, source_target_pairs={{0,8},{8,0},{16,24},{24,16},{1,9},{9,1},{17,25},{25,17},{2,10},{10... | collective-permute-start | bytes 1056776 | tf_op jit(solution)/shard_map/ppermute | solution.py:55
  37.8 19.0 %copy-start.9 = (f32[2]{0:T(128)S(1)}, f32[2]{0:T(128)}, u32[]{:S(2)}) copy-start(f32[2]{0:T(128)} %constant.15.clone) | copy-start | bytes 28
  39.5 17.3 %copy-start = (f32[128,1376]{0,1:T(8,128)S(1)}, f32[128,1376]{0,1:T(8,128)}, u32[]{:S(2)}) copy-start(f32[128,1376]{0,1:T(8,128)} %param.10) | copy-start | bytes 2113540
  39.6 17.3 %copy-start.1 = (f32[128,1376]{0,1:T(8,128)S(1)}, f32[128,1376]{0,1:T(8,128)}, u32[]{:S(2)}) copy-start(f32[128,1376]{0,1:T(8,128)} %param.11) | copy-start | bytes 2113540
  44.6 12.2 %collective-permute-start.20 = (bf16[688,128]{1,0:T(8,128)(2,1)S(1)}, bf16[688,128]{1,0:T(8,128)(2,1)S(1)}, u32[]{:S(2)}, u32[]{:S(2)}) collective-permute-start(bf16[688,128]{1,0:T(8,128)(2,1)S(1)} %pair_sum.3), channel_id=1, source_target_pairs={{0,16},{8,24},{16,0},{24,8},{1,17},{9,25},{17,1},{25,9},{2,18},{10... | collective-permute-start | bytes 528392 | tf_op jit(solution)/shard_map/ppermute | solution.py:55
  55.0 16.7 %copy-start.3 = (bf16[688,256]{1,0:T(8,128)(2,1)}, bf16[688,256]{1,0:T(8,128)(2,1)S(1)}, u32[]{:S(2)}) copy-start(bf16[688,256]{1,0:T(8,128)(2,1)S(1)} %collective-permute-done.14.met_ref.met_1) | copy-start | bytes 1056772
  55.1 15.1 %collective-permute-start.15 = (bf16[688,128]{1,0:T(8,128)(2,1)S(1)}, bf16[688,128]{1,0:T(8,128)(2,1)S(1)}, u32[]{:S(2)}, u32[]{:S(2)}) collective-permute-start(bf16[688,128]{1,0:T(8,128)(2,1)S(1)} %pair_sum.2), channel_id=1, source_target_pairs={{0,16},{8,24},{16,0},{24,8},{1,17},{9,25},{17,1},{25,9},{2,18},{10... | collective-permute-start | bytes 528392 | tf_op jit(solution)/shard_map/ppermute | solution.py:55
  56.9 24.4 %copy-start.5 = (bf16[688,128]{1,0:T(8,128)(2,1)}, bf16[688,128]{1,0:T(8,128)(2,1)S(1)}, u32[]{:S(2)}) copy-start(bf16[688,128]{1,0:T(8,128)(2,1)S(1)} %collective-permute-done.20.across_ref.across_0) | copy-start | bytes 528388
  58.4 15.5 %collective-permute-start.21 = (bf16[688,128]{1,0:T(8,128)(2,1)}, bf16[688,128]{1,0:T(8,128)(2,1)}, u32[]{:S(2)}, u32[]{:S(2)}) collective-permute-start(bf16[688,128]{1,0:T(8,128)(2,1)} %step_half.3.refs_0_), channel_id=1, source_target_pairs={{0,16},{8,24},{16,0},{24,8},{1,17},{9,25},{17,1},{25,9},{2,18},{10... | collective-permute-start | bytes 528392 | tf_op jit(solution)/shard_map/ppermute | solution.py:55
  70.2 1.5 %copy-start.7 = (bf16[688,128]{1,0:T(8,128)(2,1)}, bf16[688,128]{1,0:T(8,128)(2,1)S(1)}, u32[]{:S(2)}) copy-start(bf16[688,128]{1,0:T(8,128)(2,1)S(1)} %collective-permute-done.15.across_ref.across_1) | copy-start | bytes 528388
  71.7 9.5 %collective-permute-start.16 = (bf16[688,128]{1,0:T(8,128)(2,1)}, bf16[688,128]{1,0:T(8,128)(2,1)}, u32[]{:S(2)}, u32[]{:S(2)}) collective-permute-start(bf16[688,128]{1,0:T(8,128)(2,1)} %step_half.2.refs_0_), channel_id=1, source_target_pairs={{0,16},{8,24},{16,0},{24,8},{1,17},{9,25},{17,1},{25,9},{2,18},{10... | collective-permute-start | bytes 528392 | tf_op jit(solution)/shard_map/ppermute | solution.py:55
  71.7 18.5 %collective-permute-start.22 = (bf16[688,128]{1,0:T(8,128)(2,1)}, bf16[688,128]{1,0:T(8,128)(2,1)}, u32[]{:S(2)}, u32[]{:S(2)}) collective-permute-start(bf16[688,128]{1,0:T(8,128)(2,1)} %step_half.3.refs_0_), channel_id=1, source_target_pairs={{0,8},{8,0},{16,24},{24,16},{1,9},{9,1},{17,25},{25,17},{2,10},{10... | collective-permute-start | bytes 528392 | tf_op jit(solution)/shard_map/ppermute | solution.py:55
  73.9 16.3 %collective-permute-start.23 = (bf16[688,128]{1,0:T(8,128)(2,1)}, bf16[688,128]{1,0:T(8,128)(2,1)}, u32[]{:S(2)}, u32[]{:S(2)}) collective-permute-start(bf16[688,128]{1,0:T(8,128)(2,1)} %collective-permute-done.21.refs_1_), channel_id=1, source_target_pairs={{0,8},{8,0},{16,24},{24,16},{1,9},{9,1},{17,25},{25,17},{2,10},{10... | collective-permute-start | bytes 528392 | tf_op jit(solution)/shard_map/ppermute | solution.py:55
  74.8 18.4 %collective-permute-start.17 = (bf16[688,128]{1,0:T(8,128)(2,1)}, bf16[688,128]{1,0:T(8,128)(2,1)}, u32[]{:S(2)}, u32[]{:S(2)}) collective-permute-start(bf16[688,128]{1,0:T(8,128)(2,1)} %step_half.2.refs_0_), channel_id=1, source_target_pairs={{0,8},{8,0},{16,24},{24,16},{1,9},{9,1},{17,25},{25,17},{2,10},{10... | collective-permute-start | bytes 528392 | tf_op jit(solution)/shard_map/ppermute | solution.py:55
  81.2 12.0 %collective-permute-start.18 = (bf16[688,128]{1,0:T(8,128)(2,1)}, bf16[688,128]{1,0:T(8,128)(2,1)}, u32[]{:S(2)}, u32[]{:S(2)}) collective-permute-start(bf16[688,128]{1,0:T(8,128)(2,1)} %collective-permute-done.16.refs_1_), channel_id=1, source_target_pairs={{0,8},{8,0},{16,24},{24,16},{1,9},{9,1},{17,25},{25,17},{2,10},{10... | collective-permute-start | bytes 528392 | tf_op jit(solution)/shard_map/ppermute | solution.py:55
  85.0 1.1 %copy-start.2 = (f32[128,1376]{0,1:T(8,128)S(1)}, f32[128,1376]{0,1:T(8,128)}, u32[]{:S(2)}) copy-start(f32[128,1376]{0,1:T(8,128)} %param.11) | copy-start | bytes 2113540
  86.1 1.0 %copy-start.4 = (bf16[688,256]{1,0:T(8,128)(2,1)S(1)}, bf16[688,256]{1,0:T(8,128)(2,1)}, u32[]{:S(2)}) copy-start(bf16[688,256]{1,0:T(8,128)(2,1)} %copy-done.3) | copy-start | bytes 1056772
  87.1 0.9 copy-start.6
  88.0 0.9 copy-start.8

commit v2 on v1

--- a/solution.py
+++ b/solution.py
@@ -144,39 +144,40 @@
     )(cot_t)
 
 
-def token_sum(cots, blocks, masks, total, halves):
+def token_sum(cots, blocks, masks, total, halves, base=0):
     f_half = cots[0].shape[0]
-    f_local = 2 * f_half
+    parts = len(cots)
+    f_local = parts * f_half
     rows, cols = blocks[0].shape
     n = len(blocks)
     has_total = total is not None
     tile = TOKEN_TILE if f_half % TOKEN_TILE == 0 else f_half
 
-    def kernel(cot_0, cot_1, *refs):
-        projected, rest = refs[:n], refs[n:]
+    def kernel(*refs):
+        cot_refs, projected, rest = refs[:parts], refs[parts : parts + n], refs[parts + n :]
         me = lax.axis_index("tensor")
         odd = me % 2
         tokens = [lanes_of(me ^ (even + odd * (uneven - even)), rows) for even, uneven in masks]
         p = jnp.concatenate([ref[...] for ref in projected], axis=0)
         for start in range(0, f_local, tile):
             here, within = pl.ds(start, tile), pl.ds(start % f_half, tile)
-            cot = (cot_0, cot_1)[start // f_half]
+            cot = cot_refs[start // f_half]
             c = jnp.concatenate([cot[within, t] for t in tokens], axis=1)
             acc = jnp.dot(c, p, preferred_element_type=F32)
             if has_total:
-                acc += rest[0][here, :]
+                acc += rest[0][pl.ds(base + start, tile), :]
             if halves:
-                rest[-2 + start // f_half][within, :] = acc.astype(BF16)
+                rest[start // f_half - parts][within, :] = acc.astype(BF16)
             else:
                 rest[-1][here, :] = acc
 
     if halves:
-        out_shape = [jax.ShapeDtypeStruct((f_half, cols), BF16)] * 2
+        out_shape = [jax.ShapeDtypeStruct((f_half, cols), BF16)] * parts
     else:
         out_shape = [jax.ShapeDtypeStruct((f_local, cols), F32)]
     out = pl.pallas_call(
         kernel,
-        in_specs=[IN_VMEM] * (2 + n + has_total),
+        in_specs=[IN_VMEM] * (parts + n + has_total),
         out_specs=[IN_VMEM] * len(out_shape),
         out_shape=out_shape,
         cost_estimate=pl.CostEstimate(
@@ -332,8 +333,13 @@
         near = [own, partner, far, other_far]
         total = token_sum(cots, near, MASKS[:4], None, False)
         rest = [far_partner, other_far_partner, corner, other_corner]
-        sums.append(token_sum(cots, rest, MASKS[4:], total, s == "a"))
-    to_send, kept = sums
+        if s == "a":
+            for h in range(2):
+                base = h * cots[0].shape[0]
+                sums += token_sum([cots[h]], rest, MASKS[4:], total, True, base)
+        else:
+            sums.append(token_sum(cots, rest, MASKS[4:], total, False))
+    *to_send, kept = sums
 
     met = [swap(to_send[h], "dp", 1) for h in range(2)]
     across = [swap(pair_sum(kept, met[h], h), "dp", 2) for h in range(2)]

time: 96.6 us -> 99.1 us (1.026)
  waiting for transfers between devices: 35.1 us -> 38.3 us
    ppermute x18, waiting for transfers between devices: 28.7 us -> 32.4 us  [swap(): lax.ppermute(x, axis, [(i, i ^ mask) for i in range(lax.axis_size(axis))])]
    ppermute x6, starting transfers between devices: 11.5 us -> 10.1 us  [swap_by_core(): lax.ppermute(x, 'tensor', [(i, i ^ masks[i % 2]) for i in range(lax.axis_...]
    pallas_call x4 -> x5, Pallas kernels: 6.64 us -> 6.79 us  [token_sum(): pl.pallas_call(kernel, in_specs=[IN_VMEM] * (parts + n + has_total), out_...]
where the time goes in v2:
time: 99.1 us; the launch traced here: 98.6 us
  waiting for transfers between devices  38.3 us (39%)
  Pallas kernels  26.8 us (27%)
  starting transfers between devices  24.3 us (25%)
  local copies, waits for them, and re-layouts  7.7 us (8%)
  between operations  1.5 us (2%)
    ppermute x18, waiting for transfers between devices, swap(): lax.ppermute(x, axis, [(i, i ^ mask) for i in range(lax.axis_size(axis))])  32.4 us
    ppermute x18, starting transfers between devices, swap(): lax.ppermute(x, axis, [(i, i ^ mask) for i in range(lax.axis_size(axis))])  14.2 us
    ppermute x6, starting transfers between devices, swap_by_core(): lax.ppermute(x, 'tensor', [(i, i ^ masks[i % 2]) for i in range(lax.axis_...  10.1 us
    pallas_call x5, Pallas kernels, token_sum(): pl.pallas_call(kernel, in_specs=[IN_VMEM] * (parts + n + has_total), out_...  6.79 us
    pallas_call x2, Pallas kernels, apply_steps(): pl.pallas_call(kernel, in_specs=[IN_VMEM] * 5 + [ANYWHERE] * (out is not...  5.94 us
    ppermute x6, waiting for transfers between devices, swap_by_core(): lax.ppermute(x, 'tensor', [(i, i ^ masks[i % 2]) for i in range(lax.axis_...  5.85 us
    unnamed x21, local copies, waits for them, and re-layouts  5.43 us
    pallas_call x2, Pallas kernels, load(): pl.pallas_call(kernel, in_specs=[ANYWHERE], out_specs=IN_VMEM, out_shape=...  5.21 us
  transfers between devices with their start and end apart: 24, of which 8 were waited for; matrix products, arithmetic and copies ran while one was open for 4% of the time, Pallas kernels for 20%

profile of v2, /device:TPU:0, one launch (start us, length us, event | category | flops | bytes accessed | tf_op | source)
XLA Modules:
  0.0 98.6 jit_solution(16956975307791326242)
XLA Ops:
  0.6 4.5 %project.1 = (bf16[512,256]{1,0:T(8,128)(2,1)S(1)}, bf16[512,256]{1,0:T(8,128)(2,1)S(1)}) custom-call(bf16[512,4096]{1,0:T(8,128)(2,1)} %a_hbm.1, bf16[4096,512]{1,0:T(8,128)(2,1)} %w_hbm.1), custom_call_target="tpu_custom_call" | custom-call | flops 2147483648 | bytes 8388608 | tf_op jit(solution)/shard_map/project/pallas_call | solution.py:103
  5.1 0.6 collective-permute-start.7
  5.7 2.6 %collective-permute-start.10 = (bf16[512,256]{1,0:T(8,128)(2,1)S(1)}, bf16[512,256]{1,0:T(8,128)(2,1)S(1)}, u32[]{:S(2)}, u32[]{:S(2)}) collective-permute-start(bf16[512,256]{1,0:T(8,128)(2,1)S(1)} %get-tuple-element.8.refs_2_), channel_id=1, source_target_pairs={{0,2},{1,5},{2,0},{3,7},{4,6},{5,1},{6,4},{7,3},{8,10},{9,13},{10,... | collective-permute-start | bytes 786440 | tf_op jit(solution)/shard_map/ppermute | solution.py:59
  8.2 0.2 collective-permute-start
  8.4 1.5 %collective-permute-start.3 = (bf16[512,256]{1,0:T(8,128)(2,1)S(1)}, bf16[512,256]{1,0:T(8,128)(2,1)S(1)}, u32[]{:S(2)}, u32[]{:S(2)}) collective-permute-start(bf16[512,256]{1,0:T(8,128)(2,1)S(1)} %get-tuple-element.7.refs_2_), channel_id=1, source_target_pairs={{0,2},{1,5},{2,0},{3,7},{4,6},{5,1},{6,4},{7,3},{8,10},{9,13},{10,... | collective-permute-start | bytes 786440 | tf_op jit(solution)/shard_map/ppermute | solution.py:59
  9.9 0.0 collective-permute-done.7.refs_3_
  9.9 0.5 collective-permute-start.8
  10.4 2.1 %collective-permute-done.10.refs_4_ = bf16[512,256]{1,0:T(8,128)(2,1)S(1)} collective-permute-done((bf16[512,256]{1,0:T(8,128)(2,1)S(1)}, bf16[512,256]{1,0:T(8,128)(2,1)S(1)}, u32[]{:S(2)}, u32[]{:S(2)}) %collective-permute-start.10) | collective-permute-done | bytes 262176 | tf_op jit(solution)/shard_map/ppermute | solution.py:59
  12.6 2.0 %collective-permute-start.11 = (bf16[512,256]{1,0:T(8,128)(2,1)S(1)}, bf16[512,256]{1,0:T(8,128)(2,1)S(1)}, u32[]{:S(2)}, u32[]{:S(2)}) collective-permute-start(bf16[512,256]{1,0:T(8,128)(2,1)S(1)} %collective-permute-done.10.refs_4_), channel_id=1, source_target_pairs={{0,4},{1,3},{2,6},{3,1},{4,0},{5,7},{6,2},{7,5},{8,12},{9,11},{10,... | collective-permute-start | bytes 786440 | tf_op jit(solution)/shard_map/ppermute | solution.py:59
  14.6 0.0 collective-permute-done.refs_3_
  14.6 1.5 %collective-permute-start.1 = (bf16[512,256]{1,0:T(8,128)(2,1)S(1)}, bf16[512,256]{1,0:T(8,128)(2,1)S(1)}, u32[]{:S(2)}, u32[]{:S(2)}) collective-permute-start(bf16[512,256]{1,0:T(8,128)(2,1)S(1)} %collective-permute-done.refs_3_), channel_id=1, source_target_pairs={{0,2},{1,5},{2,0},{3,7},{4,6},{5,1},{6,4},{7,3},{8,10},{9,13},{10,... | collective-permute-start | bytes 786440 | tf_op jit(solution)/shard_map/ppermute | solution.py:59
  16.1 0.0 collective-permute-done.3.refs_4_
  16.1 1.9 %collective-permute-start.4 = (bf16[512,256]{1,0:T(8,128)(2,1)S(1)}, bf16[512,256]{1,0:T(8,128)(2,1)S(1)}, u32[]{:S(2)}, u32[]{:S(2)}) collective-permute-start(bf16[512,256]{1,0:T(8,128)(2,1)S(1)} %collective-permute-done.3.refs_4_), channel_id=1, source_target_pairs={{0,4},{1,3},{2,6},{3,1},{4,0},{5,7},{6,2},{7,5},{8,12},{9,11},{10,... | collective-permute-start | bytes 786440 | tf_op jit(solution)/shard_map/ppermute | solution.py:59
  18.1 3.3 %collective-permute-done.8.refs_1_ = bf16[512,256]{1,0:T(8,128)(2,1)S(1)} collective-permute-done((bf16[512,256]{1,0:T(8,128)(2,1)S(1)}, bf16[512,256]{1,0:T(8,128)(2,1)S(1)}, u32[]{:S(2)}, u32[]{:S(2)}) %collective-permute-start.8) | collective-permute-done | bytes 262176 | tf_op jit(solution)/shard_map/ppermute | solution.py:59
  21.3 0.4 collective-permute-done.11.refs_3_
  21.8 0.1 collective-permute-start.12
  21.9 2.6 %load.2.refs_0_ = bf16[688,4096]{1,0:T(8,128)(2,1)S(1)} custom-call(bf16[1376,4096]{1,0:T(8,128)(2,1)} %bitcast.16), custom_call_target="tpu_custom_call" | custom-call | flops 5636096 | bytes 11272192 | tf_op jit(solution)/shard_map/load/pallas_call | solution.py:133
  24.5 2.6 %load.3.refs_1_.refs_0_ = bf16[688,4096]{1,0:T(8,128)(2,1)S(1)} custom-call(bf16[1376,4096]{1,0:T(8,128)(2,1)} %bitcast.17), custom_call_target="tpu_custom_call" | custom-call | flops 5636096 | bytes 11272192 | tf_op jit(solution)/shard_map/load/pallas_call | solution.py:133
  27.1 0.0 collective-permute-done.1.refs_2_
  27.1 0.5 collective-permute-start.6
  27.6 0.0 collective-permute-done.4.refs_4_
  27.6 0.1 collective-permute-start.2
  27.7 0.0 collective-permute-done.13.refs_5_
  27.7 0.4 collective-permute-start.5
  28.1 1.6 %token_sum.7.refs_5_ = f32[1376,256]{1,0:T(8,128)S(1)} custom-call(bf16[688,4096]{1,0:T(8,128)(2,1)S(1)} %load.2.refs_0_, bf16[688,4096]{1,0:T(8,128)(2,1)S(1)} %load.3.refs_1_.refs_0_, bf16[512,256]{1,0:T(8,128)(2,1)S(1)} %get-tuple-element.8.refs_2_, bf16[512,256]{1,0:T(8,128)(2,1)S(1)} %collective-permute-done.7.refs_3_, ...), custom_call_target="tpu_custom_call" | custom-call | flops 1442840576 | bytes 8093696 | tf_op jit(solution)/shard_map/token_sum/pallas_call | solution.py:178
  29.8 0.0 collective-permute-done.9.refs_2_
  29.8 0.9 token_sum.8
  30.7 2.2 %collective-permute-start.14 = (bf16[688,256]{1,0:T(8,128)(2,1)S(1)}, bf16[688,256]{1,0:T(8,128)(2,1)S(1)}, u32[]{:S(2)}, u32[]{:S(2)}) collective-permute-start(bf16[688,256]{1,0:T(8,128)(2,1)S(1)} %token_sum.8), channel_id=1, source_target_pairs={{0,8},{8,0},{16,24},{24,16},{1,9},{9,1},{17,25},{25,17},{2,10},{10... | collective-permute-start | bytes 1056776 | tf_op jit(solution)/shard_map/ppermute | solution.py:55
  32.9 0.9 token_sum.9
  33.8 0.1 collective-permute-start.19
  34.5 0.0 collective-permute-done.6.refs_5_
  34.5 1.7 %token_sum.5.refs_6_ = f32[1376,256]{1,0:T(8,128)S(1)} custom-call(bf16[688,4096]{1,0:T(8,128)(2,1)S(1)} %load.2.refs_0_, bf16[688,4096]{1,0:T(8,128)(2,1)S(1)} %load.3.refs_1_.refs_0_, bf16[512,256]{1,0:T(8,128)(2,1)S(1)} %get-tuple-element.7.refs_2_, bf16[512,256]{1,0:T(8,128)(2,1)S(1)} %collective-permute-done.refs_3_, ...), custom_call_target="tpu_custom_call" | custom-call | flops 1442840576 | bytes 8093696 | tf_op jit(solution)/shard_map/token_sum/pallas_call | solution.py:178
  36.2 0.0 copy-start.9
  36.2 0.0 collective-permute-done.2.refs_3_
  36.2 0.0 collective-permute-done.5.refs_5_
  36.2 1.7 %token_sum.6.kept_ref = f32[1376,256]{1,0:T(8,128)S(1)} custom-call(bf16[688,4096]{1,0:T(8,128)(2,1)S(1)} %load.2.refs_0_, bf16[688,4096]{1,0:T(8,128)(2,1)S(1)} %load.3.refs_1_.refs_0_, bf16[512,256]{1,0:T(8,128)(2,1)S(1)} %collective-permute-done.1.refs_2_, bf16[512,256]{1,0:T(8,128)(2,1)S(1)} %collective-permute-done.2.refs_3_, ...), custom_call_target="tpu_custom_call" | custom-call | flops 1442840576 | bytes 8093696 | tf_op jit(solution)/shard_map/token_sum/pallas_call | solution.py:178
  37.9 0.0 copy-start
  37.9 0.0 copy-start.1
  37.9 4.0 %collective-permute-done.14.met_ref.met_1 = bf16[688,256]{1,0:T(8,128)(2,1)S(1)} collective-permute-done((bf16[688,256]{1,0:T(8,128)(2,1)S(1)}, bf16[688,256]{1,0:T(8,128)(2,1)S(1)}, u32[]{:S(2)}, u32[]{:S(2)}) %collective-permute-start.14) | collective-permute-done | bytes 352288 | tf_op jit(solution)/shard_map/ppermute | solution.py:55
  42.0 3.1 %collective-permute-start.15 = (bf16[688,128]{1,0:T(8,128)(2,1)S(1)}, bf16[688,128]{1,0:T(8,128)(2,1)S(1)}, u32[]{:S(2)}, u32[]{:S(2)}) collective-permute-start(bf16[688,128]{1,0:T(8,128)(2,1)S(1)} %pair_sum.2), channel_id=1, source_target_pairs={{0,16},{8,24},{16,0},{24,8},{1,17},{9,25},{17,1},{25,9},{2,18},{10... | collective-permute-start | bytes 528392 | tf_op jit(solution)/shard_map/ppermute | solution.py:55
  45.1 7.9 %collective-permute-done.19.met_ref.met_0 = bf16[688,256]{1,0:T(8,128)(2,1)S(1)} collective-permute-done((bf16[688,256]{1,0:T(8,128)(2,1)S(1)}, bf16[688,256]{1,0:T(8,128)(2,1)S(1)}, u32[]{:S(2)}, u32[]{:S(2)}) %collective-permute-start.19) | collective-permute-done | bytes 352288 | tf_op jit(solution)/shard_map/ppermute | solution.py:55
  53.0 1.9 %collective-permute-start.20 = (bf16[688,128]{1,0:T(8,128)(2,1)S(1)}, bf16[688,128]{1,0:T(8,128)(2,1)S(1)}, u32[]{:S(2)}, u32[]{:S(2)}) collective-permute-start(bf16[688,128]{1,0:T(8,128)(2,1)S(1)} %pair_sum.3), channel_id=1, source_target_pairs={{0,16},{8,24},{16,0},{24,8},{1,17},{9,25},{17,1},{25,9},{2,18},{10... | collective-permute-start | bytes 528392 | tf_op jit(solution)/shard_map/ppermute | solution.py:55
  55.0 9.0 %collective-permute-done.20.across_ref.across_0 = bf16[688,128]{1,0:T(8,128)(2,1)S(1)} collective-permute-done((bf16[688,128]{1,0:T(8,128)(2,1)S(1)}, bf16[688,128]{1,0:T(8,128)(2,1)S(1)}, u32[]{:S(2)}, u32[]{:S(2)}) %collective-permute-start.20) | collective-permute-done | bytes 176160 | tf_op jit(solution)/shard_map/ppermute | solution.py:55
  64.0 1.5 %step_half.3.refs_0_ = bf16[688,128]{1,0:T(8,128)(2,1)} custom-call(f32[2]{0:T(128)S(1)} %subtract_divide_fusion.scale, f32[1376,256]{1,0:T(8,128)S(1)} %token_sum.6.kept_ref, bf16[688,256]{1,0:T(8,128)(2,1)S(1)} %collective-permute-done.19.met_ref.met_0, bf16[688,128]{1,0:T(8,128)(2,1)S(1)} %collective-permute-done.20.across_ref.across_0, ...), custom_call_target="tpu_custom_call" | custom-call | flops 1761280 | bytes 1585152 | tf_op jit(solution)/shard_map/step_half/pallas_call | solution.py:234
  65.5 0.0 collective-permute-start.21
  65.5 0.0 collective-permute-done.15.across_ref.across_1
  65.5 1.5 %step_half.2.refs_0_ = bf16[688,128]{1,0:T(8,128)(2,1)} custom-call(f32[2]{0:T(128)S(1)} %subtract_divide_fusion.scale, f32[1376,256]{1,0:T(8,128)S(1)} %token_sum.6.kept_ref, bf16[688,256]{1,0:T(8,128)(2,1)S(1)} %collective-permute-done.14.met_ref.met_1, bf16[688,128]{1,0:T(8,128)(2,1)S(1)} %collective-permute-done.15.across_ref.across_1, ...), custom_call_target="tpu_custom_call" | custom-call | flops 1761280 | bytes 1585152 | tf_op jit(solution)/shard_map/step_half/pallas_call | solution.py:234
  67.0 2.9 %collective-permute-start.16 = (bf16[688,128]{1,0:T(8,128)(2,1)}, bf16[688,128]{1,0:T(8,128)(2,1)}, u32[]{:S(2)}, u32[]{:S(2)}) collective-permute-start(bf16[688,128]{1,0:T(8,128)(2,1)} %step_half.2.refs_0_), channel_id=1, source_target_pairs={{0,16},{8,24},{16,0},{24,8},{1,17},{9,25},{17,1},{25,9},{2,18},{10... | collective-permute-start | bytes 528392 | tf_op jit(solution)/shard_map/ppermute | solution.py:55
  69.9 0.2 collective-permute-start.22
  70.1 10.5 %collective-permute-done.21.refs_1_ = bf16[688,128]{1,0:T(8,128)(2,1)} collective-permute-done((bf16[688,128]{1,0:T(8,128)(2,1)}, bf16[688,128]{1,0:T(8,128)(2,1)}, u32[]{:S(2)}, u32[]{:S(2)}) %collective-permute-start.21) | collective-permute-done | bytes 176160 | tf_op jit(solution)/shard_map/ppermute | solution.py:55
  80.6 2.0 %collective-permute-start.17 = (bf16[688,128]{1,0:T(8,128)(2,1)}, bf16[688,128]{1,0:T(8,128)(2,1)}, u32[]{:S(2)}, u32[]{:S(2)}) collective-permute-start(bf16[688,128]{1,0:T(8,128)(2,1)} %step_half.2.refs_0_), channel_id=1, source_target_pairs={{0,8},{8,0},{16,24},{24,16},{1,9},{9,1},{17,25},{25,17},{2,10},{10... | collective-permute-start | bytes 528392 | tf_op jit(solution)/shard_map/ppermute | solution.py:55
  82.6 1.0 %collective-permute-done.16.refs_1_ = bf16[688,128]{1,0:T(8,128)(2,1)} collective-permute-done((bf16[688,128]{1,0:T(8,128)(2,1)}, bf16[688,128]{1,0:T(8,128)(2,1)}, u32[]{:S(2)}, u32[]{:S(2)}) %collective-permute-start.16) | collective-permute-done | bytes 176160 | tf_op jit(solution)/shard_map/ppermute | solution.py:55
  83.6 2.3 %constant_dynamic-slice_fusion = bf16[1024,512]{1,0:T(8,128)(2,1)} fusion(bf16[4096,512]{1,0:T(8,128)(2,1)} %w_hbm.1, s32[]{:T(128)S(6)} %select_n.3), kind=kLoop, calls=%fused_computation.1 | loop fusion | bytes 2097156 | tf_op jit(solution)/shard_map/dynamic_slice | solution.py:319
  85.9 1.5 %copy.12 = bf16[1024,512]{0,1:T(8,128)(2,1)S(1)} copy(bf16[1024,512]{1,0:T(8,128)(2,1)} %constant_dynamic-slice_fusion) | data formatting | bytes 2097152
  87.4 0.0 copy-start.2
  87.4 1.1 %copy-done.2 = f32[128,1376]{0,1:T(8,128)S(1)} copy-done((f32[128,1376]{0,1:T(8,128)S(1)}, f32[128,1376]{0,1:T(8,128)}, u32[]{:S(2)}) %copy-start.2) | copy-done | bytes 704536
  88.5 1.0 copy-done.4
  89.5 0.9 copy-done.6
  90.4 0.9 copy-done.8
  91.3 1.3 %moments.1 = (f32[1376,128]{1,0:T(8,128)}, f32[1376,128]{1,0:T(8,128)}) custom-call(f32[1376,256]{1,0:T(8,128)S(1)} %token_sum.6.kept_ref, bf16[688,256]{1,0:T(8,128)(2,1)S(1)} %copy-done.4, bf16[688,256]{1,0:T(8,128)(2,1)S(1)} %collective-permute-done.14.met_ref.met_1, bf16[688,128]{1,0:T(8,128)(2,1)S(1)} %copy-done.8, bf16[688,128]{1,0:T(8,128)(2,1)S(1)} %copy-done.6, ...), custom_call_target="tpu_custom_call" | custom-call | flops 1761280 | bytes 3522560 | tf_op jit(solution)/shard_map/moments/pallas_call | solution.py:256
  92.7 3.0 %apply_steps.2.refs_5_ = bf16[1376,1024]{1,0:T(8,128)(2,1)} custom-call(bf16[688,128]{1,0:T(8,128)(2,1)} %step_half.3.refs_0_, bf16[688,128]{1,0:T(8,128)(2,1)} %collective-permute-done.21.refs_1_, bf16[688,128]{1,0:T(8,128)(2,1)} %collective-permute-done.22.refs_2_, bf16[688,128]{1,0:T(8,128)(2,1)} %collective-permute-done.23.refs_3_, ...), custom_call_target="tpu_custom_call" | custom-call | flops 721420288 | bytes 3162112 | tf_op jit(solution)/shard_map/apply_steps/pallas_call | solution.py:290
  95.6 0.0 collective-permute-done.17.refs_2_
  95.6 0.0 collective-permute-done.18.refs_3_
  95.6 3.0 %apply_steps.3 = bf16[1376,1024]{1,0:T(8,128)(2,1)} custom-call(bf16[688,128]{1,0:T(8,128)(2,1)} %step_half.2.refs_0_, bf16[688,128]{1,0:T(8,128)(2,1)} %collective-permute-done.16.refs_1_, bf16[688,128]{1,0:T(8,128)(2,1)} %collective-permute-done.17.refs_2_, bf16[688,128]{1,0:T(8,128)(2,1)} %collective-permute-done.18.refs_3_, ...), custom_call_target="tpu_custom_call", output_to_operand_aliasing={{}: (5, {})} | custom-call | flops 721420288 | bytes 3162112 | tf_op jit(solution)/shard_map/apply_steps/pallas_call | solution.py:290
  (22 shorter events, 0.1 us)
Async XLA Ops:
  5.1 4.8 %collective-permute-start.7 = (bf16[512,256]{1,0:T(8,128)(2,1)S(1)}, bf16[512,256]{1,0:T(8,128)(2,1)S(1)}, u32[]{:S(2)}, u32[]{:S(2)}) collective-permute-start(bf16[512,256]{1,0:T(8,128)(2,1)S(1)} %get-tuple-element.8.refs_2_), channel_id=1, source_target_pairs={{0,1},{1,0},{2,3},{3,2},{4,5},{5,4},{6,7},{7,6},{8,9},{9,8},{10,11... | collective-permute-start | bytes 786440 | tf_op jit(solution)/shard_map/ppermute | solution.py:55
  5.7 6.9 %collective-permute-start.10 = (bf16[512,256]{1,0:T(8,128)(2,1)S(1)}, bf16[512,256]{1,0:T(8,128)(2,1)S(1)}, u32[]{:S(2)}, u32[]{:S(2)}) collective-permute-start(bf16[512,256]{1,0:T(8,128)(2,1)S(1)} %get-tuple-element.8.refs_2_), channel_id=1, source_target_pairs={{0,2},{1,5},{2,0},{3,7},{4,6},{5,1},{6,4},{7,3},{8,10},{9,13},{10,... | collective-permute-start | bytes 786440 | tf_op jit(solution)/shard_map/ppermute | solution.py:59
  8.2 6.4 %collective-permute-start = (bf16[512,256]{1,0:T(8,128)(2,1)S(1)}, bf16[512,256]{1,0:T(8,128)(2,1)S(1)}, u32[]{:S(2)}, u32[]{:S(2)}) collective-permute-start(bf16[512,256]{1,0:T(8,128)(2,1)S(1)} %get-tuple-element.7.refs_2_), channel_id=1, source_target_pairs={{0,1},{1,0},{2,3},{3,2},{4,5},{5,4},{6,7},{7,6},{8,9},{9,8},{10,11... | collective-permute-start | bytes 786440 | tf_op jit(solution)/shard_map/ppermute | solution.py:55
  8.4 7.7 %collective-permute-start.3 = (bf16[512,256]{1,0:T(8,128)(2,1)S(1)}, bf16[512,256]{1,0:T(8,128)(2,1)S(1)}, u32[]{:S(2)}, u32[]{:S(2)}) collective-permute-start(bf16[512,256]{1,0:T(8,128)(2,1)S(1)} %get-tuple-element.7.refs_2_), channel_id=1, source_target_pairs={{0,2},{1,5},{2,0},{3,7},{4,6},{5,1},{6,4},{7,3},{8,10},{9,13},{10,... | collective-permute-start | bytes 786440 | tf_op jit(solution)/shard_map/ppermute | solution.py:59
  9.9 11.4 %collective-permute-start.8 = (bf16[512,256]{1,0:T(8,128)(2,1)S(1)}, bf16[512,256]{1,0:T(8,128)(2,1)S(1)}, u32[]{:S(2)}, u32[]{:S(2)}) collective-permute-start(bf16[512,256]{1,0:T(8,128)(2,1)S(1)} %collective-permute-done.7.refs_3_), channel_id=1, source_target_pairs={{0,2},{1,5},{2,0},{3,7},{4,6},{5,1},{6,4},{7,3},{8,10},{9,13},{10,... | collective-permute-start | bytes 786440 | tf_op jit(solution)/shard_map/ppermute | solution.py:59
  12.6 9.2 %collective-permute-start.11 = (bf16[512,256]{1,0:T(8,128)(2,1)S(1)}, bf16[512,256]{1,0:T(8,128)(2,1)S(1)}, u32[]{:S(2)}, u32[]{:S(2)}) collective-permute-start(bf16[512,256]{1,0:T(8,128)(2,1)S(1)} %collective-permute-done.10.refs_4_), channel_id=1, source_target_pairs={{0,4},{1,3},{2,6},{3,1},{4,0},{5,7},{6,2},{7,5},{8,12},{9,11},{10,... | collective-permute-start | bytes 786440 | tf_op jit(solution)/shard_map/ppermute | solution.py:59
  14.6 12.5 %collective-permute-start.1 = (bf16[512,256]{1,0:T(8,128)(2,1)S(1)}, bf16[512,256]{1,0:T(8,128)(2,1)S(1)}, u32[]{:S(2)}, u32[]{:S(2)}) collective-permute-start(bf16[512,256]{1,0:T(8,128)(2,1)S(1)} %collective-permute-done.refs_3_), channel_id=1, source_target_pairs={{0,2},{1,5},{2,0},{3,7},{4,6},{5,1},{6,4},{7,3},{8,10},{9,13},{10,... | collective-permute-start | bytes 786440 | tf_op jit(solution)/shard_map/ppermute | solution.py:59
  16.1 11.5 %collective-permute-start.4 = (bf16[512,256]{1,0:T(8,128)(2,1)S(1)}, bf16[512,256]{1,0:T(8,128)(2,1)S(1)}, u32[]{:S(2)}, u32[]{:S(2)}) collective-permute-start(bf16[512,256]{1,0:T(8,128)(2,1)S(1)} %collective-permute-done.3.refs_4_), channel_id=1, source_target_pairs={{0,4},{1,3},{2,6},{3,1},{4,0},{5,7},{6,2},{7,5},{8,12},{9,11},{10,... | collective-permute-start | bytes 786440 | tf_op jit(solution)/shard_map/ppermute | solution.py:59
  18.1 9.6 %collective-permute-start.13 = (bf16[512,256]{1,0:T(8,128)(2,1)S(1)}, bf16[512,256]{1,0:T(8,128)(2,1)S(1)}, u32[]{:S(2)}, u32[]{:S(2)}) collective-permute-start(bf16[512,256]{1,0:T(8,128)(2,1)S(1)} %collective-permute-done.10.refs_4_), channel_id=1, source_target_pairs={{0,1},{1,0},{2,3},{3,2},{4,5},{5,4},{6,7},{7,6},{8,9},{9,8},{10,11... | collective-permute-start | bytes 786440 | tf_op jit(solution)/shard_map/ppermute | solution.py:55
  21.3 8.4 %collective-permute-start.9 = (bf16[512,256]{1,0:T(8,128)(2,1)S(1)}, bf16[512,256]{1,0:T(8,128)(2,1)S(1)}, u32[]{:S(2)}, u32[]{:S(2)}) collective-permute-start(bf16[512,256]{1,0:T(8,128)(2,1)S(1)} %collective-permute-done.8.refs_1_), channel_id=1, source_target_pairs={{0,1},{1,0},{2,3},{3,2},{4,5},{5,4},{6,7},{7,6},{8,9},{9,8},{10,11... | collective-permute-start | bytes 786440 | tf_op jit(solution)/shard_map/ppermute | solution.py:55
  21.8 8.0 %collective-permute-start.12 = (bf16[512,256]{1,0:T(8,128)(2,1)S(1)}, bf16[512,256]{1,0:T(8,128)(2,1)S(1)}, u32[]{:S(2)}, u32[]{:S(2)}) collective-permute-start(bf16[512,256]{1,0:T(8,128)(2,1)S(1)} %collective-permute-done.11.refs_3_), channel_id=1, source_target_pairs={{0,1},{1,0},{2,3},{3,2},{4,5},{5,4},{6,7},{7,6},{8,9},{9,8},{10,11... | collective-permute-start | bytes 786440 | tf_op jit(solution)/shard_map/ppermute | solution.py:55
  27.1 7.4 %collective-permute-start.6 = (bf16[512,256]{1,0:T(8,128)(2,1)S(1)}, bf16[512,256]{1,0:T(8,128)(2,1)S(1)}, u32[]{:S(2)}, u32[]{:S(2)}) collective-permute-start(bf16[512,256]{1,0:T(8,128)(2,1)S(1)} %collective-permute-done.3.refs_4_), channel_id=1, source_target_pairs={{0,1},{1,0},{2,3},{3,2},{4,5},{5,4},{6,7},{7,6},{8,9},{9,8},{10,11... | collective-permute-start | bytes 786440 | tf_op jit(solution)/shard_map/ppermute | solution.py:55
  27.6 8.6 %collective-permute-start.2 = (bf16[512,256]{1,0:T(8,128)(2,1)S(1)}, bf16[512,256]{1,0:T(8,128)(2,1)S(1)}, u32[]{:S(2)}, u32[]{:S(2)}) collective-permute-start(bf16[512,256]{1,0:T(8,128)(2,1)S(1)} %collective-permute-done.1.refs_2_), channel_id=1, source_target_pairs={{0,1},{1,0},{2,3},{3,2},{4,5},{5,4},{6,7},{7,6},{8,9},{9,8},{10,11... | collective-permute-start | bytes 786440 | tf_op jit(solution)/shard_map/ppermute | solution.py:55
  27.7 8.5 %collective-permute-start.5 = (bf16[512,256]{1,0:T(8,128)(2,1)S(1)}, bf16[512,256]{1,0:T(8,128)(2,1)S(1)}, u32[]{:S(2)}, u32[]{:S(2)}) collective-permute-start(bf16[512,256]{1,0:T(8,128)(2,1)S(1)} %collective-permute-done.4.refs_4_), channel_id=1, source_target_pairs={{0,1},{1,0},{2,3},{3,2},{4,5},{5,4},{6,7},{7,6},{8,9},{9,8},{10,11... | collective-permute-start | bytes 786440 | tf_op jit(solution)/shard_map/ppermute | solution.py:55
  30.7 11.2 %collective-permute-start.14 = (bf16[688,256]{1,0:T(8,128)(2,1)S(1)}, bf16[688,256]{1,0:T(8,128)(2,1)S(1)}, u32[]{:S(2)}, u32[]{:S(2)}) collective-permute-start(bf16[688,256]{1,0:T(8,128)(2,1)S(1)} %token_sum.8), channel_id=1, source_target_pairs={{0,8},{8,0},{16,24},{24,16},{1,9},{9,1},{17,25},{25,17},{2,10},{10... | collective-permute-start | bytes 1056776 | tf_op jit(solution)/shard_map/ppermute | solution.py:55
  33.8 19.2 %collective-permute-start.19 = (bf16[688,256]{1,0:T(8,128)(2,1)S(1)}, bf16[688,256]{1,0:T(8,128)(2,1)S(1)}, u32[]{:S(2)}, u32[]{:S(2)}) collective-permute-start(bf16[688,256]{1,0:T(8,128)(2,1)S(1)} %token_sum.9), channel_id=1, source_target_pairs={{0,8},{8,0},{16,24},{24,16},{1,9},{9,1},{17,25},{25,17},{2,10},{10... | collective-permute-start | bytes 1056776 | tf_op jit(solution)/shard_map/ppermute | solution.py:55
  36.2 18.8 %copy-start.9 = (f32[2]{0:T(128)S(1)}, f32[2]{0:T(128)}, u32[]{:S(2)}) copy-start(f32[2]{0:T(128)} %constant.15.clone) | copy-start | bytes 28
  37.9 26.1 %copy-start = (f32[128,1376]{0,1:T(8,128)S(1)}, f32[128,1376]{0,1:T(8,128)}, u32[]{:S(2)}) copy-start(f32[128,1376]{0,1:T(8,128)} %param.10) | copy-start | bytes 2113540
  37.9 26.1 %copy-start.1 = (f32[128,1376]{0,1:T(8,128)S(1)}, f32[128,1376]{0,1:T(8,128)}, u32[]{:S(2)}) copy-start(f32[128,1376]{0,1:T(8,128)} %param.11) | copy-start | bytes 2113540
  42.0 23.5 %collective-permute-start.15 = (bf16[688,128]{1,0:T(8,128)(2,1)S(1)}, bf16[688,128]{1,0:T(8,128)(2,1)S(1)}, u32[]{:S(2)}, u32[]{:S(2)}) collective-permute-start(bf16[688,128]{1,0:T(8,128)(2,1)S(1)} %pair_sum.2), channel_id=1, source_target_pairs={{0,16},{8,24},{16,0},{24,8},{1,17},{9,25},{17,1},{25,9},{2,18},{10... | collective-permute-start | bytes 528392 | tf_op jit(solution)/shard_map/ppermute | solution.py:55
  53.0 14.0 %copy-start.3 = (bf16[688,256]{1,0:T(8,128)(2,1)}, bf16[688,256]{1,0:T(8,128)(2,1)S(1)}, u32[]{:S(2)}) copy-start(bf16[688,256]{1,0:T(8,128)(2,1)S(1)} %collective-permute-done.19.met_ref.met_0) | copy-start | bytes 1056772
  53.0 10.9 %collective-permute-start.20 = (bf16[688,128]{1,0:T(8,128)(2,1)S(1)}, bf16[688,128]{1,0:T(8,128)(2,1)S(1)}, u32[]{:S(2)}, u32[]{:S(2)}) collective-permute-start(bf16[688,128]{1,0:T(8,128)(2,1)S(1)} %pair_sum.3), channel_id=1, source_target_pairs={{0,16},{8,24},{16,0},{24,8},{1,17},{9,25},{17,1},{25,9},{2,18},{10... | collective-permute-start | bytes 528392 | tf_op jit(solution)/shard_map/ppermute | solution.py:55
  64.0 5.9 %copy-start.7 = (bf16[688,128]{1,0:T(8,128)(2,1)}, bf16[688,128]{1,0:T(8,128)(2,1)S(1)}, u32[]{:S(2)}) copy-start(bf16[688,128]{1,0:T(8,128)(2,1)S(1)} %collective-permute-done.20.across_ref.across_0) | copy-start | bytes 528388
  65.5 15.1 %collective-permute-start.21 = (bf16[688,128]{1,0:T(8,128)(2,1)}, bf16[688,128]{1,0:T(8,128)(2,1)}, u32[]{:S(2)}, u32[]{:S(2)}) collective-permute-start(bf16[688,128]{1,0:T(8,128)(2,1)} %step_half.3.refs_0_), channel_id=1, source_target_pairs={{0,16},{8,24},{16,0},{24,8},{1,17},{9,25},{17,1},{25,9},{2,18},{10... | collective-permute-start | bytes 528392 | tf_op jit(solution)/shard_map/ppermute | solution.py:55
  65.5 18.1 %copy-start.5 = (bf16[688,128]{1,0:T(8,128)(2,1)}, bf16[688,128]{1,0:T(8,128)(2,1)S(1)}, u32[]{:S(2)}) copy-start(bf16[688,128]{1,0:T(8,128)(2,1)S(1)} %collective-permute-done.15.across_ref.across_1) | copy-start | bytes 528388
  67.0 16.6 %collective-permute-start.16 = (bf16[688,128]{1,0:T(8,128)(2,1)}, bf16[688,128]{1,0:T(8,128)(2,1)}, u32[]{:S(2)}, u32[]{:S(2)}) collective-permute-start(bf16[688,128]{1,0:T(8,128)(2,1)} %step_half.2.refs_0_), channel_id=1, source_target_pairs={{0,16},{8,24},{16,0},{24,8},{1,17},{9,25},{17,1},{25,9},{2,18},{10... | collective-permute-start | bytes 528392 | tf_op jit(solution)/shard_map/ppermute | solution.py:55
  69.9 22.7 %collective-permute-start.22 = (bf16[688,128]{1,0:T(8,128)(2,1)}, bf16[688,128]{1,0:T(8,128)(2,1)}, u32[]{:S(2)}, u32[]{:S(2)}) collective-permute-start(bf16[688,128]{1,0:T(8,128)(2,1)} %step_half.3.refs_0_), channel_id=1, source_target_pairs={{0,8},{8,0},{16,24},{24,16},{1,9},{9,1},{17,25},{25,17},{2,10},{10... | collective-permute-start | bytes 528392 | tf_op jit(solution)/shard_map/ppermute | solution.py:55
  80.6 12.1 %collective-permute-start.23 = (bf16[688,128]{1,0:T(8,128)(2,1)}, bf16[688,128]{1,0:T(8,128)(2,1)}, u32[]{:S(2)}, u32[]{:S(2)}) collective-permute-start(bf16[688,128]{1,0:T(8,128)(2,1)} %collective-permute-done.21.refs_1_), channel_id=1, source_target_pairs={{0,8},{8,0},{16,24},{24,16},{1,9},{9,1},{17,25},{25,17},{2,10},{10... | collective-permute-start | bytes 528392 | tf_op jit(solution)/shard_map/ppermute | solution.py:55
  80.6 15.0 %collective-permute-start.17 = (bf16[688,128]{1,0:T(8,128)(2,1)}, bf16[688,128]{1,0:T(8,128)(2,1)}, u32[]{:S(2)}, u32[]{:S(2)}) collective-permute-start(bf16[688,128]{1,0:T(8,128)(2,1)} %step_half.2.refs_0_), channel_id=1, source_target_pairs={{0,8},{8,0},{16,24},{24,16},{1,9},{9,1},{17,25},{25,17},{2,10},{10... | collective-permute-start | bytes 528392 | tf_op jit(solution)/shard_map/ppermute | solution.py:55
  83.6 12.0 %collective-permute-start.18 = (bf16[688,128]{1,0:T(8,128)(2,1)}, bf16[688,128]{1,0:T(8,128)(2,1)}, u32[]{:S(2)}, u32[]{:S(2)}) collective-permute-start(bf16[688,128]{1,0:T(8,128)(2,1)} %collective-permute-done.16.refs_1_), channel_id=1, source_target_pairs={{0,8},{8,0},{16,24},{24,16},{1,9},{9,1},{17,25},{25,17},{2,10},{10... | collective-permute-start | bytes 528392 | tf_op jit(solution)/shard_map/ppermute | solution.py:55
  87.4 1.1 %copy-start.2 = (f32[128,1376]{0,1:T(8,128)S(1)}, f32[128,1376]{0,1:T(8,128)}, u32[]{:S(2)}) copy-start(f32[128,1376]{0,1:T(8,128)} %param.11) | copy-start | bytes 2113540
  88.5 1.0 copy-start.4
  89.5 0.9 copy-start.6
  90.4 0.9 copy-start.8
